TPU v7x, 8 devices: a whole 2x2x1 slice. The times are simulated.
8 devices in a mesh: replica: 4 (over z, y, x), data: 2 (over core).
Axes of the slice: x: 2, y: 2, z: 1, core: 2. Of those that a mesh axis runs over, the one named last changes fastest.
Arguments:
- inp_rows: bfloat16 [32768, 768], P(('replica', 'data'))
- out_grad: bfloat16 [32768, 768], P(('replica', 'data'))
- w_up: bfloat16 [2, 768, 3072], replicated
- w_down: bfloat16 [2, 3072, 768], replicated
- master_up: float32 [2, 768, 3072], P(None, 'data')
- master_down: float32 [2, 3072, 768], P(None, 'data')
- mom_up: float32 [2, 768, 3072], P(None, 'data')
- mom_down: float32 [2, 3072, 768], P(None, 'data')
- var_up: float32 [2, 768, 3072], P(None, 'data')
- var_down: float32 [2, 3072, 768], P(None, 'data')
- clip_norm: float32 [], replicated
Outputs:
- output 1: bfloat16 [2, 768, 3072], replicated
- output 2: bfloat16 [2, 3072, 768], replicated
- output 3: float32 [2, 768, 3072], P(None, 'data')
- output 4: float32 [2, 3072, 768], P(None, 'data')
- output 5: float32 [2, 768, 3072], P(None, 'data')
- output 6: float32 [2, 3072, 768], P(None, 'data')
- output 7: float32 [2, 768, 3072], P(None, 'data')
- output 8: float32 [2, 3072, 768], P(None, 'data')
- output 9: float32 [], replicated
All inputs are finite; a program needn't handle non-finite values.
Results may differ from a plain program's by a relative error of at most 0.0110299.
Values are sent between devices in bfloat16 or wider.
A program may use at most 1 GiB of HBM per device.

v0:
```python
import jax
import jax.numpy as jnp
from jax import lax
from jax.experimental import pallas as pl
from jax.experimental.pallas import tpu as pltpu
from jax.sharding import PartitionSpec as P


BETA1 = 0.9
BETA2 = 0.95
ADAM_EPS = 1e-8
LEARN_RATE = 5e-3
NORM_EPS = 1e-6
STEP = 10
BIAS_ONE = 1.0 - BETA1 ** STEP
BIAS_TWO = 1.0 - BETA2 ** STEP
MESH = pl.DeviceIdType.MESH
F32 = jnp.float32
BF16 = jnp.bfloat16

B, D, FF = 4096, 768, 3072
NB = 6
HB = FF // NB // 2
BF = 2 * HB
R = 1024
NCH = B // R
STEPS = 2 * NB
SLOTS = 3
TAIL = 2
FULL = STEPS - TAIL
SQRT_HALF = 0.7071067811865476
PDF_SCALE = 0.3989422804014327


def gelu_value(pre_act):
    return pre_act * (0.5 + 0.5 * lax.erf(pre_act * SQRT_HALF))


def dot(a, b, dims):
    return lax.dot_general(a, b, (dims, ((), ())), preferred_element_type=F32)


class Item:
    def __init__(self, rows, cols, refs, sems):
        self.rows, self.cols = rows, cols
        self.acc, self.r0, self.r1, self.r2, self.hh = refs
        self.send, self.recv, self.loc = sems


def mega_kernel(clip_ref, h_hbm, dy_hbm, x_hbm, z_hbm, wu_hbm, wd_hbm,
                gup, gdn, gtail, stats,
                abuf, bbuf, cbuf, wa, wb, zb, slope,
                acc_d, r0_d, r1_d, r2_d, h_d,
                acc_u, r0_u, r1_u, r2_u, h_u,
                ssq, sq_in, asem, bsem, wsem, zsem, tsem, nsend, nrecv,
                send_d, recv_d, loc_d, send_u, recv_u, loc_u):
    r = lax.axis_index('replica')
    d = lax.axis_index('data')
    x = lax.rem(r, 2)
    y = lax.div(r, 2)
    x_off = 1 - 2 * x
    y_off = 2 - 4 * y
    partner = (r, 1 - d)
    n1 = (r + (1 - d) * x_off + d * y_off, d)
    n2 = (r + (1 - d) * y_off + d * x_off, d)
    a = (1 - d) * x + d * y
    b = (1 - d) * y + d * x

    item_d = Item(HB, D, (acc_d, r0_d, r1_d, r2_d, h_d), (send_d, recv_d, loc_d))
    item_u = Item(D // 2, BF, (acc_u, r0_u, r1_u, r2_u, h_u), (send_u, recv_u, loc_u))

    def rows_of(start, size):
        return pl.ds(pl.multiple_of(start, 8), size)

    def row_copy(src, dst, sem, i):
        rows = rows_of(i * R, R)
        return pltpu.make_async_copy(src.at[rows, :], dst.at[rows, :], sem.at[i])

    def w_copies(s):
        slot = lax.rem(s, 2)
        j = lax.rem(s, NB)
        ph = 1 - lax.div(s, NB)
        up, down = [], []
        for p in range(2):
            cols = pl.ds(pl.multiple_of(p * (FF // 2) + j * HB, 128), HB)
            up.append(pltpu.make_async_copy(wu_hbm.at[1, :, cols], wa.at[slot, :, p * HB:(p + 1) * HB], wsem.at[slot, p]))
            down.append(pltpu.make_async_copy(wd_hbm.at[ph, cols, :], wb.at[slot, p * HB:(p + 1) * HB, :], wsem.at[slot, 2 + p]))
        return up, down

    def z_copies(j, i):
        slot = lax.rem(i, 2)
        out = []
        for p in range(2):
            cols = pl.ds(pl.multiple_of(p * (FF // 2) + j * HB, 128), HB)
            out.append(pltpu.make_async_copy(z_hbm.at[rows_of(i * R, R), cols], zb.at[slot, :, p * HB:(p + 1) * HB], zsem.at[slot, p]))
        return out

    def g_rows(it, s, part, size):
        w = 1 - lax.div(s, NB)
        j = lax.rem(s, NB)
        if it is item_d:
            return gdn.at[w, rows_of(j * HB + part, size), :]
        return gup.at[w, j, rows_of(part, size), :]

    def cp(it, stage, s):
        k = lax.rem(s, SLOTS)
        rows = it.rows
        half, quarter = rows // 2, rows // 4
        if stage == 0:
            src, dst, dev = it.acc.at[rows_of((1 - d) * rows, rows), :], it.r0.at[k], partner
        elif stage == 1:
            src, dst, dev = it.r0.at[k, rows_of((1 - a) * half, half), :], it.r1.at[k], n1
        elif stage == 2:
            src, dst, dev = it.r1.at[k, rows_of((1 - b) * quarter, quarter), :], it.r2.at[k], n2
        elif stage == 3:
            q = rows_of(b * quarter, quarter)
            src, dst, dev = it.hh.at[k, q, :], it.hh.at[k, q, :], n2
        else:
            src, dst, dev = it.hh.at[k], g_rows(it, s, a * half, half), n1
        return pltpu.make_async_remote_copy(src_ref=src, dst_ref=dst, send_sem=it.send.at[stage, k],
                                            recv_sem=it.recv.at[stage, k], device_id=dev, device_id_type=MESH)

    def local_out(it, s):
        k = lax.rem(s, SLOTS)
        half = it.rows // 2
        return pltpu.make_async_copy(it.hh.at[k], g_rows(it, s, a * half, half), it.loc.at[k])

    def fold(it, stage, s):
        k = lax.rem(s, SLOTS)
        rows = it.rows
        half, quarter = rows // 2, rows // 4
        if stage == 0:
            return
        cp(it, stage - 1, s).wait()
        if stage == 1:
            it.r0[k] = it.r0[k] + it.acc[rows_of(d * rows, rows), :]
        elif stage == 2:
            it.r1[k] = it.r1[k] + it.r0[k, rows_of(a * half, half), :]
        elif stage == 3:
            g = (it.r2[k] + it.r1[k, rows_of(b * quarter, quarter), :]) * 0.125
            it.hh[k, rows_of(b * quarter, quarter), :] = g
            sq = g * g
            sq = sq.reshape(quarter // 8, 8, it.cols).sum(axis=0)
            tot = sq[:, :128]
            for c in range(1, it.cols // 128):
                tot = tot + sq[:, c * 128:(c + 1) * 128]
            ssq[0] += tot
        elif stage == 5:
            local_out(it, s).wait()

    def tail_out(it, s):
        k = lax.rem(s, SLOTS)
        quarter = it.rows // 4
        ty = 0 if it is item_d else 1
        return [pltpu.make_async_copy(it.hh.at[k, rows_of(b * quarter, quarter), p * 256:(p + 1) * 256],
                                      gtail.at[s - FULL, ty, p * quarter:(p + 1) * quarter, :],
                                      tsem.at[s - FULL, ty, p]) for p in range(it.cols // 256)]

    def post(it, stage, s):
        if stage == 3:
            @pl.when(s < FULL)
            def _():
                cp(it, 3, s).start()

            @pl.when(s >= FULL)
            def _():
                for c in tail_out(it, s):
                    c.start()
        elif stage < 5:
            cp(it, stage, s).start()
        if stage == 4:
            local_out(it, s).start()

    def tick(s, plan):
        late = None
        for it, stage, lag in plan:
            t = s - lag
            ok = jnp.logical_and(t >= 0, t < (FULL if stage >= 4 else STEPS))

            @pl.when(ok)
            def _():
                fold(it, stage, t)

            if late is not None:
                pit, pstage, pt, pok = late

                @pl.when(pok)
                def _():
                    post(pit, pstage, pt)
            late = (it, stage, t, ok)
        pit, pstage, pt, pok = late

        @pl.when(pok)
        def _():
            post(pit, pstage, pt)

    ssq[0] = jnp.zeros((8, 128), F32)
    for i in range(NCH):
        row_copy(h_hbm, abuf, asem, i).start()
        row_copy(dy_hbm, bbuf, bsem, i).start()
        if i == 0:
            up, down = w_copies(0)
            for c in up + down:
                c.start()

    barrier = pltpu.get_barrier_semaphore()
    for dev in (partner, n1, n2):
        pl.semaphore_signal(barrier, inc=1, device_id=dev, device_id_type=MESH)
    pl.semaphore_wait(barrier, 3)

    def zero_c(i, carry):
        cbuf[rows_of(i * 128, 128), :] = jnp.zeros((128, D), F32)
        return carry

    lax.fori_loop(0, B // 128, zero_c, 0)

    def pass_one(s):
        slot = lax.rem(s, 2)
        j = lax.rem(s, NB)
        acc_d[...] = jnp.zeros_like(acc_d)

        def chunk(i, carry):
            rows = rows_of(i * R, R)
            zs = lax.rem(i, 2)

            @pl.when(s == 0)
            def _():
                row_copy(h_hbm, abuf, asem, i).wait()
                row_copy(dy_hbm, bbuf, bsem, i).wait()

            @pl.when(s < NB)
            def _():
                zb[zs] = dot(abuf[rows, :], wa[slot], ((1,), (0,))).astype(BF16)

            @pl.when(s >= NB)
            def _():
                for c in z_copies(j, i):
                    c.wait()

                @pl.when(i + 1 < NCH)
                def _():
                    for c in z_copies(j, i + 1):
                        c.start()

            z = zb[zs].astype(F32)
            cdf = 0.5 + 0.5 * lax.erf(z * SQRT_HALF)
            slope[rows, :] = cdf + z * jnp.exp(-0.5 * z * z) * PDF_SCALE
            u = (z * cdf).astype(BF16)
            acc_d[...] += dot(u, bbuf[rows, :], ((0,), (0,)))
            return carry

        lax.fori_loop(0, NCH, chunk, 0)

    def pass_two(s):
        slot = lax.rem(s, 2)
        acc_u[...] = jnp.zeros_like(acc_u)

        def chunk(i, carry):
            rows = rows_of(i * R, R)

            @pl.when(s == NB)
            def _():
                row_copy(x_hbm, abuf, asem, i).wait()

            e = dot(bbuf[rows, :], wb[slot], ((1,), (1,))).astype(BF16)
            dd = (e.astype(F32) * slope[rows, :]).astype(BF16)
            acc_u[...] += dot(abuf[rows, :], dd, ((0,), (0,)))

            @pl.when(s < NB)
            def _():
                cbuf[rows, :] += dot(dd, wa[slot], ((1,), (1,)))

            return carry

        lax.fori_loop(0, NCH, chunk, 0)

    def step(s, carry):
        @pl.when(s == NB)
        def _():
            for i in range(NCH):
                row_copy(x_hbm, abuf, asem, i).start()

            def conv(i, carry):
                rows = rows_of(i * 128, 128)
                bbuf[rows, :] = cbuf[rows, :].astype(BF16)
                return carry

            lax.fori_loop(0, B // 128, conv, 0)

        @pl.when(s < STEPS)
        def _():
            up, down = w_copies(s)
            for c in down:
                c.wait()

            @pl.when(s < NB)
            def _():
                for c in up:
                    c.wait()

            @pl.when(s >= NB)
            def _():
                for c in z_copies(lax.rem(s, NB), 0):
                    c.start()

            @pl.when(s + 1 < STEPS)
            def _():
                up, down = w_copies(s + 1)
                for c in down:
                    c.start()

                @pl.when(s + 1 < NB)
                def _():
                    for c in up:
                        c.start()

            pass_one(s)

        tick(s, [(item_d, 2, 1), (item_u, 1, 1), (item_u, 3, 2), (item_d, 4, 2), (item_u, 5, 3), (item_d, 0, 0)])

        @pl.when(s < STEPS)
        def _():
            pass_two(s)

        tick(s, [(item_u, 2, 1), (item_d, 1, 0), (item_d, 3, 1), (item_u, 4, 2), (item_d, 5, 2), (item_u, 0, 0)])
        return carry

    lax.fori_loop(0, STEPS + 2, step, 0)

    for i, dev in enumerate((partner, (r + x_off, d), (r + y_off, d))):
        c = pltpu.make_async_remote_copy(src_ref=ssq.at[i], dst_ref=sq_in.at[i], send_sem=nsend.at[i],
                                         recv_sem=nrecv.at[i], device_id=dev, device_id_type=MESH)
        c.start()
        if i == 0:
            for t in range(FULL, STEPS):
                for it in (item_d, item_u):
                    for tc in tail_out(it, t):
                        tc.wait()
        c.wait()
        ssq[i + 1] = ssq[i] + sq_in[i]
    total = jnp.sum(ssq[3], axis=0, keepdims=True)
    total = jnp.sum(total, axis=1, keepdims=True)
    norm = jnp.sqrt(total)
    scale = jnp.minimum(1.0, clip_ref[0] / (norm + NORM_EPS))
    stats[0] = jnp.broadcast_to(norm, (8, 128))
    stats[1] = jnp.broadcast_to(scale, (8, 128))


def backward_reduce(clip, h, dy, x, z1, w_up, w_down):
    any_spec = pl.BlockSpec(memory_space=pl.ANY)
    vmem = pltpu.VMEM

    def item(rows, cols, acc):
        return [vmem(acc, F32), vmem((SLOTS, rows, cols), F32), vmem((SLOTS, rows // 2, cols), F32),
                vmem((SLOTS, rows // 4, cols), F32), vmem((SLOTS, rows // 2, cols), F32)]

    dma = pltpu.SemaphoreType.DMA
    return pl.pallas_call(
        mega_kernel,
        out_shape=(jax.ShapeDtypeStruct((2, NB, D // 2, BF), F32),
                   jax.ShapeDtypeStruct((2, FF // 2, D), F32),
                   jax.ShapeDtypeStruct((TAIL, 2, 192, 256), F32),
                   jax.ShapeDtypeStruct((2, 8, 128), F32)),
        in_specs=[pl.BlockSpec(memory_space=pltpu.SMEM)] + [any_spec] * 6,
        out_specs=(any_spec, any_spec, any_spec, pl.BlockSpec(memory_space=pltpu.VMEM)),
        scratch_shapes=[vmem((B, D), BF16), vmem((B, D), BF16), vmem((B, D), F32),
                        vmem((2, D, BF), BF16), vmem((2, BF, D), BF16), vmem((2, R, BF), BF16), vmem((B, BF), F32)]
        + item(HB, D, (BF, D)) + item(D // 2, BF, (D, BF))
        + [vmem((4, 8, 128), F32), vmem((3, 8, 128), F32)]
        + [dma((NCH,)), dma((NCH,)), dma((2, 4)), dma((2, 2)), dma((TAIL, 2, 3)), dma((3,)), dma((3,))]
        + [dma((5, SLOTS)), dma((5, SLOTS)), dma((SLOTS,))] * 2,
        compiler_params=pltpu.CompilerParams(collective_id=0, has_side_effects=True, vmem_limit_bytes=67043328),
        name='backward_reduce',
    )(clip, h, dy, x, z1, w_up, w_down)


def adam_rule(s, g, master_ref, mom_ref, var_ref, new_master_ref, new_mom_ref, new_var_ref, w_ref):
    mom = BETA1 * mom_ref[0] + (1.0 - BETA1) * s * g
    var = BETA2 * var_ref[0] + (1.0 - BETA2) * (s * s) * (g * g)
    master = master_ref[0] - LEARN_RATE * (mom / BIAS_ONE) / (jnp.sqrt(var / BIAS_TWO) + ADAM_EPS)
    new_mom_ref[0] = mom
    new_var_ref[0] = var
    new_master_ref[0] = master
    w_ref[0] = master.astype(BF16)


def adam_body(tail, n_alias, stats, *refs):
    s = stats[1, 0:1, 0:1]
    if tail:
        own, from_n2, from_n1, from_diag = refs[:4]
        refs = refs[4:]
        r = lax.axis_index('replica')
        d = lax.axis_index('data')
        x, y = lax.rem(r, 2), lax.div(r, 2)
        a = (1 - d) * x + d * y
        b = (1 - d) * y + d * x
        i = pl.program_id(0)
        half = lax.rem(i, 2)

        def pick(qa, qb, ty, rows):
            da = lax.rem(qa + a, 2)
            db = lax.rem(qb + b, 2)
            near = jnp.where(db == 0, own[0, ty, rows, :], from_n2[0, ty, rows, :])
            far = jnp.where(db == 0, from_n1[0, ty, rows, :], from_diag[0, ty, rows, :])
            return jnp.where(da == 0, near, far)

        up_rows = pl.ds(pl.multiple_of(half * 96, 8), 96)
        g_up = jnp.concatenate([pick(q // 2, q % 2, 1, up_rows) for q in range(4)], axis=0)
        g_down = jnp.concatenate([jnp.concatenate([pick(half, qb, 0, pl.ds(p * 64, 64)) for p in range(3)], axis=1)
                                  for qb in range(2)], axis=0)
    else:
        g_up = refs[0][0, 0]
        g_down = refs[1][0]
        refs = refs[2:]
    states, outs = refs[:6], refs[6 + n_alias:]
    adam_rule(s, g_up, *states[:3], *outs[:3], outs[6])
    adam_rule(s, g_down, *states[3:], *outs[3:6], outs[7])


def adam(stats, grads, states, prev, w, lo, hi, tail=False):
    any_spec = pl.BlockSpec(memory_space=pl.ANY)
    up = pl.BlockSpec((1, D // 2, HB), lambda i: (w, 0, lax.rem(i + lo, 2) * NB + lax.div(i + lo, 2)))
    down = pl.BlockSpec((1, 128, D), lambda i: (w, i + lo, 0))
    if tail:
        g_specs = [pl.BlockSpec((1, 2, 192, 256), lambda i: (lax.div(i, 2), 0, 0, 0))] * 4
    else:
        g_specs = [pl.BlockSpec((1, 1, D // 2, HB), lambda i: (w, lax.div(i + lo, 2), 0, lax.rem(i + lo, 2))), down]
    n = hi - lo
    full = [jax.ShapeDtypeStruct(v.shape, F32) for v in states]
    halves = [jax.ShapeDtypeStruct((n, D // 2, HB), BF16), jax.ShapeDtypeStruct((n, 128, D), BF16)]
    first = 1 + len(grads) + 6
    cells = n * (D // 2 * HB + 128 * D)
    return pl.pallas_call(
        lambda *refs: adam_body(tail, len(prev), *refs),
        grid=(n,),
        out_shape=full + halves,
        in_specs=[pl.BlockSpec((2, 8, 128), lambda i: (0, 0, 0))] + g_specs + [up] * 3 + [down] * 3 + [any_spec] * len(prev),
        out_specs=[up] * 3 + [down] * 3 + [pl.BlockSpec((1, D // 2, HB), lambda i: (i, 0, 0)), pl.BlockSpec((1, 128, D), lambda i: (i, 0, 0))],
        input_output_aliases={first + k: k for k in range(len(prev))},
        compiler_params=pltpu.CompilerParams(vmem_limit_bytes=67043328),
        cost_estimate=pl.CostEstimate(flops=cells * 400, bytes_accessed=cells * 30, transcendentals=0),
    )(stats, *grads, *states, *prev)


def place_kernel(w, lo, n, n_extra, own_u, own_d, got_u, got_d, *rest):
    out_u, out_d, buf_u, buf_d, sem_in, sem_out = rest[n_extra:]
    d = lax.axis_index('data')
    loads, stores = [], []
    for k, (src_u, src_d) in enumerate(((own_u, own_d), (got_u, got_d))):
        q = d if k == 0 else 1 - d
        loads.append(pltpu.make_async_copy(src_u, buf_u.at[k], sem_in.at[k, 0]))
        loads.append(pltpu.make_async_copy(src_d, buf_d.at[k], sem_in.at[k, 1]))
        for i in range(n):
            t = i + lo
            cols = pl.ds(((t % 2) * NB + t // 2) * HB, HB)
            stores.append((2 * k, pltpu.make_async_copy(
                buf_u.at[k, i], out_u.at[w, pl.ds(pl.multiple_of(q * (D // 2), 8), D // 2), cols], sem_out.at[k, i])))
            rows = pl.ds(pl.multiple_of(q * (FF // 2) + t * 128, 8), 128)
            stores.append((2 * k + 1, pltpu.make_async_copy(buf_d.at[k, i], out_d.at[w, rows, :], sem_out.at[k, n + i])))
    for c in loads:
        c.start()
    for k, c in enumerate(loads):
        c.wait()
        for kk, st in stores:
            if kk == k:
                st.start()
    for kk, st in stores:
        st.wait()


def place(w, lo, own, got, prev, after):
    n = own[0].shape[0]
    any_spec = pl.BlockSpec(memory_space=pl.ANY)
    extra = list(prev) + list(after)
    cells = 2 * n * (D // 2 * HB + 128 * D)
    return pl.pallas_call(
        lambda *refs: place_kernel(w, lo, n, len(extra), *refs),
        out_shape=(jax.ShapeDtypeStruct((2, D, FF), BF16), jax.ShapeDtypeStruct((2, FF, D), BF16)),
        in_specs=[any_spec] * (4 + len(extra)),
        out_specs=(any_spec, any_spec),
        scratch_shapes=[pltpu.VMEM((2, n, D // 2, HB), BF16), pltpu.VMEM((2, n, 128, D), BF16),
                        pltpu.SemaphoreType.DMA((2, 2)), pltpu.SemaphoreType.DMA((2, 2 * n))],
        input_output_aliases={4 + k: k for k in range(len(prev))},
        compiler_params=pltpu.CompilerParams(vmem_limit_bytes=67043328),
        cost_estimate=pl.CostEstimate(flops=cells * 100, bytes_accessed=cells * 4, transcendentals=0),
    )(*own, *got, *extra)


def swap(halves):
    return [lax.ppermute(v, 'data', [(0, 1), (1, 0)]) for v in halves]


def solution(mesh):
    batch_spec = P(('replica', 'data'), None)
    whole_spec = P()
    shard_spec = P(None, 'data', None)
    first_axis = [(r * 2 + d, (r ^ (1 if d == 0 else 2)) * 2 + d) for r in range(4) for d in range(2)]
    second_axis = [(r * 2 + d, (r ^ (2 if d == 0 else 1)) * 2 + d) for r in range(4) for d in range(2)]
    both_axes = [(r * 2 + d, (r ^ 3) * 2 + d) for r in range(4) for d in range(2)]

    def device_step(inp_rows, out_grad, w_up, w_down, master_up, master_down, mom_up, mom_down, var_up, var_down, clip_norm):
        pre_one = jnp.dot(inp_rows, w_up[0], preferred_element_type=F32).astype(BF16)
        act_one = gelu_value(pre_one.astype(F32)).astype(BF16)
        mid_rows = jnp.dot(act_one, w_down[0], preferred_element_type=F32).astype(BF16)
        g_up, g_down, g_tail, stats = backward_reduce(clip_norm.reshape(1), mid_rows, out_grad, inp_rows, pre_one, w_up, w_down)
        axes = ('replica', 'data')
        tails = [g_tail]
        for perm in (second_axis, first_axis, both_axes):
            tails.append(lax.ppermute(g_tail, axes, perm))
        states = [master_up, mom_up, var_up, master_down, mom_down, var_down]
        cut = 2 * (NB - TAIL)
        *new, wu, wd = adam(stats, [g_up, g_down], states, [], 1, 0, 2 * NB)
        own_a = [wu, wd]
        got_a = swap(own_a)
        *new, wu, wd = adam(stats, [g_up, g_down], states, new, 0, 0, cut)
        own_b = [wu, wd]
        got_b = swap(own_b)
        weights = place(1, 0, own_a, got_a, [], [wu])
        *new, wu, wd = adam(stats, tails, states, new, 0, cut, 2 * NB, tail=True)
        own_c = [wu, wd]
        got_c = swap(own_c)
        weights = place(0, 0, own_b, got_b, weights, [wu])
        weights = place(0, cut, own_c, got_c, weights, [])
        m_up, o_up, v_up, m_down, o_down, v_down = new
        return (weights[0], weights[1], m_up, m_down, o_up, o_down, v_up, v_down, stats[0, 0, 0])

    return jax.shard_map(device_step, mesh=mesh, in_specs=(batch_spec, batch_spec, whole_spec, whole_spec, shard_spec, shard_spec, shard_spec, shard_spec, shard_spec, shard_spec, whole_spec), out_specs=(whole_spec, whole_spec, shard_spec, shard_spec, shard_spec, shard_spec, shard_spec, shard_spec, whole_spec), check_vma=False)
```

profile of v0, /device:TPU:0, one launch (start us, length us, event | category | flops | bytes accessed | tf_op | source)
XLA Modules:
  0.0 490.6 jit_solution(17102726142859739314)
XLA Ops:
  1.3 0.0 copy-start
  1.3 27.0 %convolution_convert_fusion.z_hbm = bf16[4096,3072]{1,0:T(8,128)(2,1)} fusion(bf16[4096,768]{1,0:T(8,128)(2,1)} %x_hbm.1, bf16[2,768,3072]{2,1,0:T(8,128)(2,1)} %wu_hbm.1), kind=kOutput, calls=%fused_computation.7 | convolution fusion | flops 19339935744 | bytes 36175872 | tf_op jit(solution)/shard_map/dot_general | solution.py:502
  28.3 0.0 copy-done
  28.3 29.9 %fusion.6.h_hbm = bf16[4096,768]{1,0:T(8,128)(2,1)} fusion(bf16[4096,3072]{1,0:T(8,128)(2,1)} %convolution_convert_fusion.z_hbm, bf16[2,3072,768]{2,1,0:T(8,128)(2,1)S(1)} %copy-done), kind=kOutput, calls=%fused_computation.8 | convolution fusion | flops 19405996032 | bytes 36175872 | tf_op jit(solution)/shard_map/dot_general | solution.py:504
  58.2 338.8 %backward_reduce.1 = (f32[2,6,384,512]{3,2,1,0:T(8,128)}, f32[2,1536,768]{2,1,0:T(8,128)}, f32[2,2,192,256]{3,2,1,0:T(8,128)}, f32[2,8,128]{2,1,0:T(8,128)}) custom-call(f32[1]{0:T(128)} %bitcast.12.clip_ref, bf16[4096,768]{1,0:T(8,128)(2,1)} %fusion.6.h_hbm, bf16[4096,768]{1,0:T(8,128)(2,1)} %dy_hbm.1, bf16[4096,768]{1,0:T(8,128)(2,1)} %x_hbm.1, ...), custom_call_target="tpu_custom_call" | custom-call | tf_op jit(solution)/shard_map/backward_reduce/pallas_call | solution.py:358
  397.0 26.4 %shard_map.178 = (f32[2,384,3072]{2,1,0:T(8,128)}, f32[2,384,3072]{2,1,0:T(8,128)}, f32[2,384,3072]{2,1,0:T(8,128)}, f32[2,1536,768]{2,1,0:T(8,128)}, f32[2,1536...) custom-call(f32[2,8,128]{2,1,0:T(8,128)} %get-tuple-element.43.refs_0_, ...), custom_call_target="tpu_custom_call" | custom-call | flops 943718400 | bytes 70778880 | tf_op jit(solution)/shard_map/pallas_call | solution.py:433
  423.5 0.0 collective-permute-start.7
  423.5 0.5 collective-permute-start.8
  424.0 1.1 collective-permute-start
  425.1 2.2 collective-permute-start.1
  427.3 0.4 collective-permute-start.2
  427.7 17.9 %shard_map.179 = (f32[2,384,3072]{2,1,0:T(8,128)}, f32[2,384,3072]{2,1,0:T(8,128)}, f32[2,384,3072]{2,1,0:T(8,128)}, f32[2,1536,768]{2,1,0:T(8,128)}, f32[2,1536...) custom-call(f32[2,8,128]{2,1,0:T(8,128)} %get-tuple-element.43.refs_, ...), custom_call_target="tpu_custom_call", output_to_operand_aliasing={{0}: (9, {}), {1}: (10, {}), {2}: (11, {}), {3}: (12, {}), ... | custom-call | flops 629145600 | bytes 47185920 | tf_op jit(solution)/shard_map/pallas_call | solution.py:433
  445.6 0.0 collective-permute-done.refs_2_
  445.6 0.0 collective-permute-start.5
  445.7 0.4 collective-permute-done.1.refs_3_
  446.0 0.1 collective-permute-start.6
  446.2 15.5 %collective-permute-done.2.refs_4_ = f32[2,2,192,256]{3,2,1,0:T(8,128)} collective-permute-done((f32[2,2,192,256]{3,2,1,0:T(8,128)}, f32[2,2,192,256]{3,2,1,0:T(8,128)}, u32[]{:S(2)}, u32[]{:S(2)}) %collective-permute-start.2) | collective-permute-done | bytes 786464 | tf_op jit(solution)/shard_map/ppermute | solution.py:509
  461.6 10.6 %shard_map.180 = (f32[2,384,3072]{2,1,0:T(8,128)}, f32[2,384,3072]{2,1,0:T(8,128)}, f32[2,384,3072]{2,1,0:T(8,128)}, f32[2,1536,768]{2,1,0:T(8,128)}, f32[2,1536...) custom-call(f32[2,8,128]{2,1,0:T(8,128)} %get-tuple-element.43.refs_, ...), custom_call_target="tpu_custom_call", output_to_operand_aliasing={{0}: (11, {}), {1}: (12, {}), {2}: (13, {}), {3}: (14, {}),... | custom-call | flops 314572800 | bytes 23592960 | tf_op jit(solution)/shard_map/pallas_call | solution.py:433
  472.3 0.0 collective-permute-start.3
  472.3 0.0 collective-permute-done.7.refs_2_
  472.3 0.5 collective-permute-start.4
  472.8 1.2 slice.11
  474.0 0.0 collective-permute-done.8.refs_3_
  474.0 8.1 %shard_map.181 = (bf16[2,768,3072]{2,1,0:T(8,128)(2,1)}, bf16[2,3072,768]{2,1,0:T(8,128)(2,1)}) custom-call(bf16[12,384,256]{2,1,0:T(8,128)(2,1)} %get-tuple-element.63.refs_0_, bf16[12,128,768]{2,1,0:T(8,128)(2,1)} %get-tuple-element.64.refs_1_, bf16[12,384,256]{2,1,0:T(8,128)(2,1)} %collective-permute-done.7.refs_2_, ...), custom_call_target="tpu_custom_call" | custom-call | flops 471859200 | bytes 18874368 | tf_op jit(solution)/shard_map/pallas_call | solution.py:476
  482.1 0.0 collective-permute-done.5.refs_2_
  482.1 0.0 collective-permute-done.6.refs_3_
  482.1 5.4 %shard_map.182 = (bf16[2,768,3072]{2,1,0:T(8,128)(2,1)}, bf16[2,3072,768]{2,1,0:T(8,128)(2,1)}) custom-call(bf16[8,384,256]{2,1,0:T(8,128)(2,1)} %get-tuple-element.61.refs_4_.refs_0_, bf16[8,128,768]{2,1,0:T(8,128)(2,1)} %get-tuple-element.62.refs_1_, ...), custom_call_target="tpu_custom_call", output_to_operand_aliasing={{0}: (4, {}), {1}: (5, {})} | custom-call | flops 314572800 | bytes 12582912 | tf_op jit(solution)/shard_map/pallas_call | solution.py:476
  487.5 0.0 collective-permute-done.3.refs_2_
  487.5 0.0 collective-permute-done.4.refs_3_
  487.5 3.0 shard_map.183
Async XLA Ops:
  1.3 27.0 %copy-start = (bf16[2,3072,768]{2,1,0:T(8,128)(2,1)S(1)}, bf16[2,3072,768]{2,1,0:T(8,128)(2,1)}, u32[]{:S(2)}) copy-start(bf16[2,3072,768]{2,1,0:T(8,128)(2,1)} %wd_hbm.1) | copy-start | bytes 28311556
  423.5 48.8 %collective-permute-start.7 = (bf16[12,384,256]{2,1,0:T(8,128)(2,1)}, bf16[12,384,256]{2,1,0:T(8,128)(2,1)}, u32[]{:S(2)}, u32[]{:S(2)}) collective-permute-start(bf16[12,384,256]{2,1,0:T(8,128)(2,1)} %get-tuple-element.63.refs_0_), channel_id=1, source_target_pairs={{0,1},{1,0},{2,3},{3,2},{4,5},{5,4},{6,7},{7,6}} | collective-permute-start | bytes 7077896 | tf_op jit(solution)/shard_map/ppermute | solution.py:490
  423.5 50.5 %collective-permute-start.8 = (bf16[12,128,768]{2,1,0:T(8,128)(2,1)}, bf16[12,128,768]{2,1,0:T(8,128)(2,1)}, u32[]{:S(2)}, u32[]{:S(2)}) collective-permute-start(bf16[12,128,768]{2,1,0:T(8,128)(2,1)} %get-tuple-element.64.refs_1_), channel_id=1, source_target_pairs={{0,1},{1,0},{2,3},{3,2},{4,5},{5,4},{6,7},{7,6}} | collective-permute-start | bytes 7077896 | tf_op jit(solution)/shard_map/ppermute | solution.py:490
  424.0 21.6 %collective-permute-start = (f32[2,2,192,256]{3,2,1,0:T(8,128)}, f32[2,2,192,256]{3,2,1,0:T(8,128)}, u32[]{:S(2)}, u32[]{:S(2)}) collective-permute-start(f32[2,2,192,256]{3,2,1,0:T(8,128)} %get-tuple-element.44.refs_1_), channel_id=1, source_target_pairs={{0,4},{1,3},{2,6},{3,1},{4,0},{5,7},{6,2},{7,5}} | collective-permute-start | bytes 2359304 | tf_op jit(solution)/shard_map/ppermute | solution.py:509
  425.1 21.0 %collective-permute-start.1 = (f32[2,2,192,256]{3,2,1,0:T(8,128)}, f32[2,2,192,256]{3,2,1,0:T(8,128)}, u32[]{:S(2)}, u32[]{:S(2)}) collective-permute-start(f32[2,2,192,256]{3,2,1,0:T(8,128)} %get-tuple-element.44.refs_1_), channel_id=1, source_target_pairs={{0,2},{1,5},{2,0},{3,7},{4,6},{5,1},{6,4},{7,3}} | collective-permute-start | bytes 2359304 | tf_op jit(solution)/shard_map/ppermute | solution.py:509
  427.3 34.3 %collective-permute-start.2 = (f32[2,2,192,256]{3,2,1,0:T(8,128)}, f32[2,2,192,256]{3,2,1,0:T(8,128)}, u32[]{:S(2)}, u32[]{:S(2)}) collective-permute-start(f32[2,2,192,256]{3,2,1,0:T(8,128)} %get-tuple-element.44.refs_1_), channel_id=1, source_target_pairs={{0,6},{1,7},{2,4},{3,5},{4,2},{5,3},{6,0},{7,1}} | collective-permute-start | bytes 2359304 | tf_op jit(solution)/shard_map/ppermute | solution.py:509
  445.6 36.4 %collective-permute-start.5 = (bf16[8,384,256]{2,1,0:T(8,128)(2,1)}, bf16[8,384,256]{2,1,0:T(8,128)(2,1)}, u32[]{:S(2)}, u32[]{:S(2)}) collective-permute-start(bf16[8,384,256]{2,1,0:T(8,128)(2,1)} %get-tuple-element.61.refs_4_.refs_0_), channel_id=1, source_target_pairs={{0,1},{1,0},{2,3},{3,2},{4,5},{5,4},{6,7},{7,6}} | collective-permute-start | bytes 4718600 | tf_op jit(solution)/shard_map/ppermute | solution.py:490
  446.0 36.0 %collective-permute-start.6 = (bf16[8,128,768]{2,1,0:T(8,128)(2,1)}, bf16[8,128,768]{2,1,0:T(8,128)(2,1)}, u32[]{:S(2)}, u32[]{:S(2)}) collective-permute-start(bf16[8,128,768]{2,1,0:T(8,128)(2,1)} %get-tuple-element.62.refs_1_), channel_id=1, source_target_pairs={{0,1},{1,0},{2,3},{3,2},{4,5},{5,4},{6,7},{7,6}} | collective-permute-start | bytes 4718600 | tf_op jit(solution)/shard_map/ppermute | solution.py:490
  472.3 15.2 %collective-permute-start.3 = (bf16[4,384,256]{2,1,0:T(8,128)(2,1)}, bf16[4,384,256]{2,1,0:T(8,128)(2,1)}, u32[]{:S(2)}, u32[]{:S(2)}) collective-permute-start(bf16[4,384,256]{2,1,0:T(8,128)(2,1)} %get-tuple-element.59.refs_6_.refs_0_), channel_id=1, source_target_pairs={{0,1},{1,0},{2,3},{3,2},{4,5},{5,4},{6,7},{7,6}} | collective-permute-start | bytes 2359304 | tf_op jit(solution)/shard_map/ppermute | solution.py:490
  472.3 15.2 %collective-permute-start.4 = (bf16[4,128,768]{2,1,0:T(8,128)(2,1)}, bf16[4,128,768]{2,1,0:T(8,128)(2,1)}, u32[]{:S(2)}, u32[]{:S(2)}) collective-permute-start(bf16[4,128,768]{2,1,0:T(8,128)(2,1)} %get-tuple-element.60.refs_1_), channel_id=1, source_target_pairs={{0,1},{1,0},{2,3},{3,2},{4,5},{5,4},{6,7},{7,6}} | collective-permute-start | bytes 2359304 | tf_op jit(solution)/shard_map/ppermute | solution.py:490
where the time goes:
time: 491 us
  Pallas kernels  410 us (84%)
  matrix products  56.9 us (12%)
  waiting for transfers between devices  15.9 us (3%)
  starting transfers between devices  4.93 us (1%)
    pallas_call x1, Pallas kernels, backward_reduce(): pl.pallas_call(mega_kernel, out_shape=(jax.ShapeDtypeStruct((2, NB, D //...  339 us
    pallas_call x3, Pallas kernels, adam(): pl.pallas_call(lambda *refs: adam_body(tail, len(prev), *refs), grid=(n,)...  54.9 us
    dot_general x1, matrix products, device_step(): jnp.dot(act_one, w_down[0], preferred_element_type=F32).astype(BF16)  29.9 us
    dot_general x1, matrix products, device_step(): jnp.dot(inp_rows, w_up[0], preferred_element_type=F32).astype(BF16)  27 us
    pallas_call x3, Pallas kernels, place(): pl.pallas_call(lambda *refs: place_kernel(w, lo, n, len(extra), *refs), o...  16.4 us
    ppermute x3, waiting for transfers between devices, device_step(): tails.append(lax.ppermute(g_tail, axes, perm))  15.9 us
  transfers between devices with their start and end apart: 9, of which 2 were waited for; matrix products, arithmetic and copies ran while one was open for 0% of the time, Pallas kernels for 9%

commit v1 on v0

--- a/solution.py
+++ b/solution.py
@@ -22,14 +22,15 @@
 NB = 6
 HB = FF // NB // 2
 BF = 2 * HB
-R = 1024
+R = B // 2
 NCH = B // R
 STEPS = 2 * NB
 SLOTS = 3
-TAIL = 2
+TAIL = 3
 FULL = STEPS - TAIL
 SQRT_HALF = 0.7071067811865476
 PDF_SCALE = 0.3989422804014327
+EXP_SCALE = -0.5 * 1.4426950408889634
 
 
 def gelu_value(pre_act):
@@ -49,7 +50,7 @@
 
 def mega_kernel(clip_ref, h_hbm, dy_hbm, x_hbm, z_hbm, wu_hbm, wd_hbm,
                 gup, gdn, gtail, stats,
-                abuf, bbuf, cbuf, wa, wb, zb, slope,
+                abuf, bbuf, cbuf, wa, wb, zb,
                 acc_d, r0_d, r1_d, r2_d, h_d,
                 acc_u, r0_u, r1_u, r2_u, h_u,
                 ssq, sq_in, asem, bsem, wsem, zsem, tsem, nsend, nrecv,
@@ -87,12 +88,13 @@
             down.append(pltpu.make_async_copy(wd_hbm.at[ph, cols, :], wb.at[slot, p * HB:(p + 1) * HB, :], wsem.at[slot, 2 + p]))
         return up, down
 
-    def z_copies(j, i):
-        slot = lax.rem(i, 2)
+    def z_copies(s, i):
+        j = lax.rem(s, NB)
         out = []
         for p in range(2):
             cols = pl.ds(pl.multiple_of(p * (FF // 2) + j * HB, 128), HB)
-            out.append(pltpu.make_async_copy(z_hbm.at[rows_of(i * R, R), cols], zb.at[slot, :, p * HB:(p + 1) * HB], zsem.at[slot, p]))
+            rows = rows_of(i * R, R)
+            out.append(pltpu.make_async_copy(z_hbm.at[rows, cols], zb.at[rows, p * HB:(p + 1) * HB], zsem.at[i, p]))
         return out
 
     def g_rows(it, s, part, size):
@@ -214,80 +216,93 @@
 
     lax.fori_loop(0, B // 128, zero_c, 0)
 
-    def pass_one(s):
+    def gelu_dot(zf, rows):
+        u = (zf * (0.5 + 0.5 * lax.erf(zf * SQRT_HALF))).astype(BF16)
+        acc_d[...] += dot(u, bbuf[rows, :], ((0,), (0,)))
+
+    def pass_one(s, i):
         slot = lax.rem(s, 2)
-        j = lax.rem(s, NB)
-        acc_d[...] = jnp.zeros_like(acc_d)
-
-        def chunk(i, carry):
-            rows = rows_of(i * R, R)
-            zs = lax.rem(i, 2)
-
+        rows = rows_of(i * R, R)
+
+        @pl.when(i == 0)
+        def _():
+            acc_d[...] = jnp.zeros_like(acc_d)
+
+        @pl.when(s < NB)
+        def _():
             @pl.when(s == 0)
             def _():
                 row_copy(h_hbm, abuf, asem, i).wait()
                 row_copy(dy_hbm, bbuf, bsem, i).wait()
 
-            @pl.when(s < NB)
-            def _():
-                zb[zs] = dot(abuf[rows, :], wa[slot], ((1,), (0,))).astype(BF16)
-
-            @pl.when(s >= NB)
-            def _():
-                for c in z_copies(j, i):
-                    c.wait()
-
-                @pl.when(i + 1 < NCH)
-                def _():
-                    for c in z_copies(j, i + 1):
-                        c.start()
-
-            z = zb[zs].astype(F32)
-            cdf = 0.5 + 0.5 * lax.erf(z * SQRT_HALF)
-            slope[rows, :] = cdf + z * jnp.exp(-0.5 * z * z) * PDF_SCALE
-            u = (z * cdf).astype(BF16)
-            acc_d[...] += dot(u, bbuf[rows, :], ((0,), (0,)))
-            return carry
-
-        lax.fori_loop(0, NCH, chunk, 0)
-
-    def pass_two(s):
+            z = dot(abuf[rows, :], wa[slot], ((1,), (0,))).astype(BF16)
+            zb[rows, :] = z
+            gelu_dot(z.astype(F32), rows)
+
+        @pl.when(s >= NB)
+        def _():
+            for c in z_copies(s, i):
+                c.wait()
+            gelu_dot(zb[rows, :].astype(F32), rows)
+
+    def slope_dot(s, rows):
         slot = lax.rem(s, 2)
-        acc_u[...] = jnp.zeros_like(acc_u)
-
-        def chunk(i, carry):
-            rows = rows_of(i * R, R)
-
+        e = dot(bbuf[rows, :], wb[slot], ((1,), (1,))).astype(BF16)
+        zf = zb[rows, :].astype(F32)
+        slope = 0.5 + 0.5 * lax.erf(zf * SQRT_HALF) + zf * jnp.exp2(zf * zf * EXP_SCALE) * PDF_SCALE
+        dd = (e.astype(F32) * slope).astype(BF16)
+        acc_u[...] += dot(abuf[rows, :], dd, ((0,), (0,)))
+        return dd
+
+    def pass_two(s, i):
+        slot = lax.rem(s, 2)
+        rows = rows_of(i * R, R)
+
+        @pl.when(i == 0)
+        def _():
+            acc_u[...] = jnp.zeros_like(acc_u)
+
+        @pl.when(s < NB)
+        def _():
+            dd = slope_dot(s, rows)
+            cbuf[rows, :] += dot(dd, wa[slot], ((1,), (1,)))
+
+        @pl.when(s >= NB)
+        def _():
             @pl.when(s == NB)
             def _():
                 row_copy(x_hbm, abuf, asem, i).wait()
 
-            e = dot(bbuf[rows, :], wb[slot], ((1,), (1,))).astype(BF16)
-            dd = (e.astype(F32) * slope[rows, :]).astype(BF16)
-            acc_u[...] += dot(abuf[rows, :], dd, ((0,), (0,)))
-
-            @pl.when(s < NB)
-            def _():
-                cbuf[rows, :] += dot(dd, wa[slot], ((1,), (1,)))
-
-            return carry
-
-        lax.fori_loop(0, NCH, chunk, 0)
-
-    def step(s, carry):
-        @pl.when(s == NB)
-        def _():
-            for i in range(NCH):
-                row_copy(x_hbm, abuf, asem, i).start()
-
-            def conv(i, carry):
-                rows = rows_of(i * 128, 128)
+            slope_dot(s, rows)
+
+        @pl.when(jnp.logical_and(s + 1 >= NB, s + 1 < STEPS))
+        def _():
+            for c in z_copies(s + 1, i):
+                c.start()
+
+    plans = (((item_d, 2, 1), (item_d, 4, 2)),
+             ((item_u, 1, 1), (item_u, 3, 2), (item_u, 5, 3), (item_d, 0, 0)),
+             ((item_d, 1, 0), (item_d, 3, 1), (item_d, 5, 2)),
+             ((item_u, 2, 1), (item_u, 4, 2), (item_u, 0, 0)))
+
+    def quarter(t, carry):
+        s = lax.div(t, 4)
+        pos = lax.rem(t, 4)
+        i = lax.rem(pos, 2)
+
+        @pl.when(t == 4 * NB)
+        def _():
+            for k in range(NCH):
+                row_copy(x_hbm, abuf, asem, k).start()
+
+            def conv(k, carry):
+                rows = rows_of(k * 128, 128)
                 bbuf[rows, :] = cbuf[rows, :].astype(BF16)
                 return carry
 
             lax.fori_loop(0, B // 128, conv, 0)
 
-        @pl.when(s < STEPS)
+        @pl.when(jnp.logical_and(pos == 0, s < STEPS))
         def _():
             up, down = w_copies(s)
             for c in down:
@@ -297,11 +312,6 @@
             def _():
                 for c in up:
                     c.wait()
-
-            @pl.when(s >= NB)
-            def _():
-                for c in z_copies(lax.rem(s, NB), 0):
-                    c.start()
 
             @pl.when(s + 1 < STEPS)
             def _():
@@ -314,18 +324,21 @@
                     for c in up:
                         c.start()
 
-            pass_one(s)
-
-        tick(s, [(item_d, 2, 1), (item_u, 1, 1), (item_u, 3, 2), (item_d, 4, 2), (item_u, 5, 3), (item_d, 0, 0)])
-
-        @pl.when(s < STEPS)
-        def _():
-            pass_two(s)
-
-        tick(s, [(item_u, 2, 1), (item_d, 1, 0), (item_d, 3, 1), (item_u, 4, 2), (item_d, 5, 2), (item_u, 0, 0)])
+        @pl.when(jnp.logical_and(pos < 2, s < STEPS))
+        def _():
+            pass_one(s, i)
+
+        @pl.when(jnp.logical_and(pos >= 2, s < STEPS))
+        def _():
+            pass_two(s, i)
+
+        for k, plan in enumerate(plans):
+            @pl.when(pos == k)
+            def _():
+                tick(s, plan)
         return carry
 
-    lax.fori_loop(0, STEPS + 2, step, 0)
+    lax.fori_loop(0, 4 * (STEPS + 1) + 2, quarter, 0)
 
     for i, dev in enumerate((partner, (r + x_off, d), (r + y_off, d))):
         c = pltpu.make_async_remote_copy(src_ref=ssq.at[i], dst_ref=sq_in.at[i], send_sem=nsend.at[i],
@@ -364,10 +377,10 @@
         in_specs=[pl.BlockSpec(memory_space=pltpu.SMEM)] + [any_spec] * 6,
         out_specs=(any_spec, any_spec, any_spec, pl.BlockSpec(memory_space=pltpu.VMEM)),
         scratch_shapes=[vmem((B, D), BF16), vmem((B, D), BF16), vmem((B, D), F32),
-                        vmem((2, D, BF), BF16), vmem((2, BF, D), BF16), vmem((2, R, BF), BF16), vmem((B, BF), F32)]
+                        vmem((2, D, BF), BF16), vmem((2, BF, D), BF16), vmem((B, BF), BF16)]
         + item(HB, D, (BF, D)) + item(D // 2, BF, (D, BF))
         + [vmem((4, 8, 128), F32), vmem((3, 8, 128), F32)]
-        + [dma((NCH,)), dma((NCH,)), dma((2, 4)), dma((2, 2)), dma((TAIL, 2, 3)), dma((3,)), dma((3,))]
+        + [dma((NCH,)), dma((NCH,)), dma((2, 4)), dma((NCH, 2)), dma((TAIL, 2, 3)), dma((3,)), dma((3,))]
         + [dma((5, SLOTS)), dma((5, SLOTS)), dma((SLOTS,))] * 2,
         compiler_params=pltpu.CompilerParams(collective_id=0, has_side_effects=True, vmem_limit_bytes=67043328),
         name='backward_reduce',

time: 491 us -> 485 us (0.988)
  Pallas kernels: 410 us -> 384 us
  waiting for transfers between devices: 15.9 us -> 36.4 us
    pallas_call x1, Pallas kernels: 339 us -> 313 us  [backward_reduce(): pl.pallas_call(mega_kernel, out_shape=(jax.ShapeDtypeStruct((2, NB, D //...]
    ppermute x3, waiting for transfers between devices: 15.9 us -> 36.4 us  [device_step(): tails.append(lax.ppermute(g_tail, axes, perm))]
  transfers between devices with their start and end apart: 9 -> 9, of which waited for: 2 -> 1; matrix products, arithmetic and copies ran while one was open for 0% -> 0% of each run, Pallas kernels for 9% -> 8%
where the time goes in v1:
time: 485 us
  Pallas kernels  384 us (79%)
  matrix products  56.9 us (12%)
  waiting for transfers between devices  36.4 us (8%)
  starting transfers between devices  5.05 us (1%)
    pallas_call x1, Pallas kernels, backward_reduce(): pl.pallas_call(mega_kernel, out_shape=(jax.ShapeDtypeStruct((2, NB, D //...  313 us
    pallas_call x3, Pallas kernels, adam(): pl.pallas_call(lambda *refs: adam_body(tail, len(prev), *refs), grid=(n,)...  55.2 us
    ppermute x3, waiting for transfers between devices, device_step(): tails.append(lax.ppermute(g_tail, axes, perm))  36.4 us
    dot_general x1, matrix products, device_step(): jnp.dot(act_one, w_down[0], preferred_element_type=F32).astype(BF16)  29.9 us
    dot_general x1, matrix products, device_step(): jnp.dot(inp_rows, w_up[0], preferred_element_type=F32).astype(BF16)  27 us
    pallas_call x3, Pallas kernels, place(): pl.pallas_call(lambda *refs: place_kernel(w, lo, n, len(extra), *refs), o...  15.9 us
  transfers between devices with their start and end apart: 9, of which 1 were waited for; matrix products, arithmetic and copies ran while one was open for 0% of the time, Pallas kernels for 8%

profile of v1, /device:TPU:0, one launch (start us, length us, event | category | flops | bytes accessed | tf_op | source)
XLA Modules:
  0.0 484.7 jit_solution(18365268368740599415)
XLA Ops:
  1.3 0.0 copy-start
  1.3 27.0 %convolution_convert_fusion.z_hbm = bf16[4096,3072]{1,0:T(8,128)(2,1)} fusion(bf16[4096,768]{1,0:T(8,128)(2,1)} %x_hbm.1, bf16[2,768,3072]{2,1,0:T(8,128)(2,1)} %wu_hbm.1), kind=kOutput, calls=%fused_computation.7 | convolution fusion | flops 19339935744 | bytes 36175872 | tf_op jit(solution)/shard_map/dot_general | solution.py:515
  28.3 0.0 copy-done
  28.3 29.9 %fusion.6.h_hbm = bf16[4096,768]{1,0:T(8,128)(2,1)} fusion(bf16[4096,3072]{1,0:T(8,128)(2,1)} %convolution_convert_fusion.z_hbm, bf16[2,3072,768]{2,1,0:T(8,128)(2,1)S(1)} %copy-done), kind=kOutput, calls=%fused_computation.8 | convolution fusion | flops 19405996032 | bytes 36175872 | tf_op jit(solution)/shard_map/dot_general | solution.py:517
  58.2 312.5 %backward_reduce.1 = (f32[2,6,384,512]{3,2,1,0:T(8,128)}, f32[2,1536,768]{2,1,0:T(8,128)}, f32[3,2,192,256]{3,2,1,0:T(8,128)}, f32[2,8,128]{2,1,0:T(8,128)}) custom-call(f32[1]{0:T(128)} %bitcast.12.clip_ref, bf16[4096,768]{1,0:T(8,128)(2,1)} %fusion.6.h_hbm, bf16[4096,768]{1,0:T(8,128)(2,1)} %dy_hbm.1, bf16[4096,768]{1,0:T(8,128)(2,1)} %x_hbm.1, ...), custom_call_target="tpu_custom_call" | custom-call | tf_op jit(solution)/shard_map/backward_reduce/pallas_call | solution.py:371
  370.7 26.3 %shard_map.178 = (f32[2,384,3072]{2,1,0:T(8,128)}, f32[2,384,3072]{2,1,0:T(8,128)}, f32[2,384,3072]{2,1,0:T(8,128)}, f32[2,1536,768]{2,1,0:T(8,128)}, f32[2,1536...) custom-call(f32[2,8,128]{2,1,0:T(8,128)} %get-tuple-element.43.refs_0_, ...), custom_call_target="tpu_custom_call" | custom-call | flops 943718400 | bytes 70778880 | tf_op jit(solution)/shard_map/pallas_call | solution.py:446
  397.1 0.0 collective-permute-start.7
  397.1 0.5 collective-permute-start.8
  397.6 0.2 collective-permute-start
  397.8 1.9 collective-permute-start.1
  399.7 1.4 collective-permute-start.2
  401.1 13.8 %shard_map.179 = (f32[2,384,3072]{2,1,0:T(8,128)}, f32[2,384,3072]{2,1,0:T(8,128)}, f32[2,384,3072]{2,1,0:T(8,128)}, f32[2,1536,768]{2,1,0:T(8,128)}, f32[2,1536...) custom-call(f32[2,8,128]{2,1,0:T(8,128)} %get-tuple-element.43.refs_, ...), custom_call_target="tpu_custom_call", output_to_operand_aliasing={{0}: (9, {}), {1}: (10, {}), {2}: (11, {}), {3}: (12, {}), ... | custom-call | flops 471859200 | bytes 35389440 | tf_op jit(solution)/shard_map/pallas_call | solution.py:446
  414.9 36.3 %collective-permute-done.refs_2_ = f32[3,2,192,256]{3,2,1,0:T(8,128)} collective-permute-done((f32[3,2,192,256]{3,2,1,0:T(8,128)}, f32[3,2,192,256]{3,2,1,0:T(8,128)}, u32[]{:S(2)}, u32[]{:S(2)}) %collective-permute-start) | collective-permute-done | bytes 1179680 | tf_op jit(solution)/shard_map/ppermute | solution.py:522
  451.2 0.0 collective-permute-start.5
  451.2 0.0 collective-permute-done.1.refs_3_
  451.2 0.5 collective-permute-start.6
  451.7 0.0 collective-permute-done.2.refs_4_
  451.7 15.1 %shard_map.180 = (f32[2,384,3072]{2,1,0:T(8,128)}, f32[2,384,3072]{2,1,0:T(8,128)}, f32[2,384,3072]{2,1,0:T(8,128)}, f32[2,1536,768]{2,1,0:T(8,128)}, f32[2,1536...) custom-call(f32[2,8,128]{2,1,0:T(8,128)} %get-tuple-element.43.refs_, ...), custom_call_target="tpu_custom_call", output_to_operand_aliasing={{0}: (11, {}), {1}: (12, {}), {2}: (13, {}), {3}: (14, {}),... | custom-call | flops 471859200 | bytes 35389440 | tf_op jit(solution)/shard_map/pallas_call | solution.py:446
  466.9 0.0 collective-permute-start.3
  466.9 0.0 collective-permute-done.7.refs_2_
  466.9 0.5 collective-permute-start.4
  467.4 1.2 slice.11
  468.6 0.0 collective-permute-done.8.refs_3_
  468.6 8.1 %shard_map.181 = (bf16[2,768,3072]{2,1,0:T(8,128)(2,1)}, bf16[2,3072,768]{2,1,0:T(8,128)(2,1)}) custom-call(bf16[12,384,256]{2,1,0:T(8,128)(2,1)} %get-tuple-element.63.refs_0_, bf16[12,128,768]{2,1,0:T(8,128)(2,1)} %get-tuple-element.64.refs_1_, bf16[12,384,256]{2,1,0:T(8,128)(2,1)} %collective-permute-done.7.refs_2_, ...), custom_call_target="tpu_custom_call" | custom-call | flops 471859200 | bytes 18874368 | tf_op jit(solution)/shard_map/pallas_call | solution.py:489
  476.7 0.0 collective-permute-done.5.refs_2_
  476.7 0.0 collective-permute-done.6.refs_3_
  476.7 3.9 shard_map.182
  480.6 0.0 collective-permute-done.3.refs_2_
  480.6 0.0 collective-permute-done.4.refs_3_
  480.6 3.9 shard_map.183
Async XLA Ops:
  1.3 27.0 %copy-start = (bf16[2,3072,768]{2,1,0:T(8,128)(2,1)S(1)}, bf16[2,3072,768]{2,1,0:T(8,128)(2,1)}, u32[]{:S(2)}) copy-start(bf16[2,3072,768]{2,1,0:T(8,128)(2,1)} %wd_hbm.1) | copy-start | bytes 28311556
  397.1 69.9 %collective-permute-start.7 = (bf16[12,384,256]{2,1,0:T(8,128)(2,1)}, bf16[12,384,256]{2,1,0:T(8,128)(2,1)}, u32[]{:S(2)}, u32[]{:S(2)}) collective-permute-start(bf16[12,384,256]{2,1,0:T(8,128)(2,1)} %get-tuple-element.63.refs_0_), channel_id=1, source_target_pairs={{0,1},{1,0},{2,3},{3,2},{4,5},{5,4},{6,7},{7,6}} | collective-permute-start | bytes 7077896 | tf_op jit(solution)/shard_map/ppermute | solution.py:503
  397.1 71.5 %collective-permute-start.8 = (bf16[12,128,768]{2,1,0:T(8,128)(2,1)}, bf16[12,128,768]{2,1,0:T(8,128)(2,1)}, u32[]{:S(2)}, u32[]{:S(2)}) collective-permute-start(bf16[12,128,768]{2,1,0:T(8,128)(2,1)} %get-tuple-element.64.refs_1_), channel_id=1, source_target_pairs={{0,1},{1,0},{2,3},{3,2},{4,5},{5,4},{6,7},{7,6}} | collective-permute-start | bytes 7077896 | tf_op jit(solution)/shard_map/ppermute | solution.py:503
  397.6 53.6 %collective-permute-start = (f32[3,2,192,256]{3,2,1,0:T(8,128)}, f32[3,2,192,256]{3,2,1,0:T(8,128)}, u32[]{:S(2)}, u32[]{:S(2)}) collective-permute-start(f32[3,2,192,256]{3,2,1,0:T(8,128)} %get-tuple-element.44.refs_1_), channel_id=1, source_target_pairs={{0,4},{1,3},{2,6},{3,1},{4,0},{5,7},{6,2},{7,5}} | collective-permute-start | bytes 3538952 | tf_op jit(solution)/shard_map/ppermute | solution.py:522
  397.8 53.4 %collective-permute-start.1 = (f32[3,2,192,256]{3,2,1,0:T(8,128)}, f32[3,2,192,256]{3,2,1,0:T(8,128)}, u32[]{:S(2)}, u32[]{:S(2)}) collective-permute-start(f32[3,2,192,256]{3,2,1,0:T(8,128)} %get-tuple-element.44.refs_1_), channel_id=1, source_target_pairs={{0,2},{1,5},{2,0},{3,7},{4,6},{5,1},{6,4},{7,3}} | collective-permute-start | bytes 3538952 | tf_op jit(solution)/shard_map/ppermute | solution.py:522
  399.7 52.0 %collective-permute-start.2 = (f32[3,2,192,256]{3,2,1,0:T(8,128)}, f32[3,2,192,256]{3,2,1,0:T(8,128)}, u32[]{:S(2)}, u32[]{:S(2)}) collective-permute-start(f32[3,2,192,256]{3,2,1,0:T(8,128)} %get-tuple-element.44.refs_1_), channel_id=1, source_target_pairs={{0,6},{1,7},{2,4},{3,5},{4,2},{5,3},{6,0},{7,1}} | collective-permute-start | bytes 3538952 | tf_op jit(solution)/shard_map/ppermute | solution.py:522
  451.2 25.5 %collective-permute-start.5 = (bf16[6,384,256]{2,1,0:T(8,128)(2,1)}, bf16[6,384,256]{2,1,0:T(8,128)(2,1)}, u32[]{:S(2)}, u32[]{:S(2)}) collective-permute-start(bf16[6,384,256]{2,1,0:T(8,128)(2,1)} %get-tuple-element.61.refs_4_.refs_0_), channel_id=1, source_target_pairs={{0,1},{1,0},{2,3},{3,2},{4,5},{5,4},{6,7},{7,6}} | collective-permute-start | bytes 3538952 | tf_op jit(solution)/shard_map/ppermute | solution.py:503
  451.2 25.5 %collective-permute-start.6 = (bf16[6,128,768]{2,1,0:T(8,128)(2,1)}, bf16[6,128,768]{2,1,0:T(8,128)(2,1)}, u32[]{:S(2)}, u32[]{:S(2)}) collective-permute-start(bf16[6,128,768]{2,1,0:T(8,128)(2,1)} %get-tuple-element.62.refs_1_), channel_id=1, source_target_pairs={{0,1},{1,0},{2,3},{3,2},{4,5},{5,4},{6,7},{7,6}} | collective-permute-start | bytes 3538952 | tf_op jit(solution)/shard_map/ppermute | solution.py:503
  466.9 13.8 %collective-permute-start.3 = (bf16[6,384,256]{2,1,0:T(8,128)(2,1)}, bf16[6,384,256]{2,1,0:T(8,128)(2,1)}, u32[]{:S(2)}, u32[]{:S(2)}) collective-permute-start(bf16[6,384,256]{2,1,0:T(8,128)(2,1)} %get-tuple-element.59.refs_6_.refs_0_), channel_id=1, source_target_pairs={{0,1},{1,0},{2,3},{3,2},{4,5},{5,4},{6,7},{7,6}} | collective-permute-start | bytes 3538952 | tf_op jit(solution)/shard_map/ppermute | solution.py:503
  466.9 13.7 %collective-permute-start.4 = (bf16[6,128,768]{2,1,0:T(8,128)(2,1)}, bf16[6,128,768]{2,1,0:T(8,128)(2,1)}, u32[]{:S(2)}, u32[]{:S(2)}) collective-permute-start(bf16[6,128,768]{2,1,0:T(8,128)(2,1)} %get-tuple-element.60.refs_1_), channel_id=1, source_target_pairs={{0,1},{1,0},{2,3},{3,2},{4,5},{5,4},{6,7},{7,6}} | collective-permute-start | bytes 3538952 | tf_op jit(solution)/shard_map/ppermute | solution.py:503

commit v2 on v1

--- a/solution.py
+++ b/solution.py
@@ -30,6 +30,7 @@
 FULL = STEPS - TAIL
 SQRT_HALF = 0.7071067811865476
 PDF_SCALE = 0.3989422804014327
+NBUF = 2
 EXP_SCALE = -0.5 * 1.4426950408889634
 
 
@@ -387,17 +388,42 @@
     )(clip, h, dy, x, z1, w_up, w_down)
 
 
-def adam_rule(s, g, master_ref, mom_ref, var_ref, new_master_ref, new_mom_ref, new_var_ref, w_ref):
+def forward_body(x, wu, wd, z_ref, h_ref):
+    z = dot(x[...], wu[0], ((1,), (0,))).astype(BF16)
+    z_ref[...] = z
+    u = gelu_value(z.astype(F32)).astype(BF16)
+    h_ref[...] = dot(u, wd[0], ((1,), (0,))).astype(BF16)
+
+
+def forward(x, w_up, w_down):
+    rows = 1024
+    once = pl.Buffered(1)
+    return pl.pallas_call(
+        forward_body,
+        grid=(B // rows,),
+        out_shape=(jax.ShapeDtypeStruct((B, FF), BF16), jax.ShapeDtypeStruct((B, D), BF16)),
+        in_specs=[pl.BlockSpec((rows, D), lambda i: (i, 0)),
+                  pl.BlockSpec((1, D, FF), lambda i: (0, 0, 0), pipeline_mode=once),
+                  pl.BlockSpec((1, FF, D), lambda i: (0, 0, 0), pipeline_mode=once)],
+        out_specs=(pl.BlockSpec((rows, FF), lambda i: (i, 0)), pl.BlockSpec((rows, D), lambda i: (i, 0))),
+        compiler_params=pltpu.CompilerParams(vmem_limit_bytes=67043328),
+        name='forward',
+    )(x, w_up, w_down)
+
+
+def adam_rule(s, g, master_ref, mom_ref, var_ref, new_master_ref, new_mom_ref, new_var_ref, w_refs):
     mom = BETA1 * mom_ref[0] + (1.0 - BETA1) * s * g
     var = BETA2 * var_ref[0] + (1.0 - BETA2) * (s * s) * (g * g)
     master = master_ref[0] - LEARN_RATE * (mom / BIAS_ONE) / (jnp.sqrt(var / BIAS_TWO) + ADAM_EPS)
     new_mom_ref[0] = mom
     new_var_ref[0] = var
     new_master_ref[0] = master
-    w_ref[0] = master.astype(BF16)
-
-
-def adam_body(tail, n_alias, stats, *refs):
+    w = master.astype(BF16)
+    for ref in w_refs:
+        ref[0] = w
+
+
+def adam_body(tail, n_alias, me, stats, *refs):
     s = stats[1, 0:1, 0:1]
     if tail:
         own, from_n2, from_n1, from_diag = refs[:4]
@@ -426,50 +452,62 @@
         g_down = refs[1][0]
         refs = refs[2:]
     states, outs = refs[:6], refs[6 + n_alias:]
-    adam_rule(s, g_up, *states[:3], *outs[:3], outs[6])
-    adam_rule(s, g_down, *states[3:], *outs[3:6], outs[7])
-
-
-def adam(stats, grads, states, prev, w, lo, hi, tail=False):
+    adam_rule(s, g_up, *states[:3], *outs[:3], (outs[6], outs[8]))
+    adam_rule(s, g_down, *states[3:], *outs[3:6], (outs[7], outs[9]))
+
+
+def adam(me, stats, grads, states, prev, w, lo, hi, tail=False):
     any_spec = pl.BlockSpec(memory_space=pl.ANY)
-    up = pl.BlockSpec((1, D // 2, HB), lambda i: (w, 0, lax.rem(i + lo, 2) * NB + lax.div(i + lo, 2)))
-    down = pl.BlockSpec((1, 128, D), lambda i: (w, i + lo, 0))
+    deep = pl.Buffered(NBUF)
+
+    def col(i):
+        return lax.rem(i + lo, 2) * NB + lax.div(i + lo, 2)
+
+    def specs(**kw):
+        up = pl.BlockSpec((1, D // 2, HB), lambda i, me: (w, 0, col(i)), **kw)
+        down = pl.BlockSpec((1, 128, D), lambda i, me: (w, i + lo, 0), **kw)
+        return [up] * 3 + [down] * 3
+
     if tail:
-        g_specs = [pl.BlockSpec((1, 2, 192, 256), lambda i: (lax.div(i, 2), 0, 0, 0))] * 4
+        g_specs = [pl.BlockSpec((1, 2, 192, 256), lambda i, me: (lax.div(i, 2), 0, 0, 0))] * 4
     else:
-        g_specs = [pl.BlockSpec((1, 1, D // 2, HB), lambda i: (w, lax.div(i + lo, 2), 0, lax.rem(i + lo, 2))), down]
+        g_specs = [pl.BlockSpec((1, 1, D // 2, HB), lambda i, me: (w, lax.div(i + lo, 2), 0, lax.rem(i + lo, 2)), pipeline_mode=deep),
+                   pl.BlockSpec((1, 128, D), lambda i, me: (w, i + lo, 0), pipeline_mode=deep)]
     n = hi - lo
     full = [jax.ShapeDtypeStruct(v.shape, F32) for v in states]
+    whole = [jax.ShapeDtypeStruct((2, D, FF), BF16), jax.ShapeDtypeStruct((2, FF, D), BF16)]
     halves = [jax.ShapeDtypeStruct((n, D // 2, HB), BF16), jax.ShapeDtypeStruct((n, 128, D), BF16)]
-    first = 1 + len(grads) + 6
+    first = 2 + len(grads) + 6
     cells = n * (D // 2 * HB + 128 * D)
     return pl.pallas_call(
         lambda *refs: adam_body(tail, len(prev), *refs),
-        grid=(n,),
-        out_shape=full + halves,
-        in_specs=[pl.BlockSpec((2, 8, 128), lambda i: (0, 0, 0))] + g_specs + [up] * 3 + [down] * 3 + [any_spec] * len(prev),
-        out_specs=[up] * 3 + [down] * 3 + [pl.BlockSpec((1, D // 2, HB), lambda i: (i, 0, 0)), pl.BlockSpec((1, 128, D), lambda i: (i, 0, 0))],
+        out_shape=full + whole + halves,
+        grid_spec=pltpu.PrefetchScalarGridSpec(
+            num_scalar_prefetch=1,
+            grid=(n,),
+            in_specs=[pl.BlockSpec((2, 8, 128), lambda i, me: (0, 0, 0))] + g_specs + specs(pipeline_mode=deep) + [any_spec] * len(prev),
+            out_specs=specs() + [pl.BlockSpec((1, D // 2, HB), lambda i, me: (w, me[0], col(i))),
+                                 pl.BlockSpec((1, 128, D), lambda i, me: (w, me[0] * (FF // 256) + i + lo, 0)),
+                                 pl.BlockSpec((1, D // 2, HB), lambda i, me: (i, 0, 0)),
+                                 pl.BlockSpec((1, 128, D), lambda i, me: (i, 0, 0))]),
         input_output_aliases={first + k: k for k in range(len(prev))},
         compiler_params=pltpu.CompilerParams(vmem_limit_bytes=67043328),
         cost_estimate=pl.CostEstimate(flops=cells * 400, bytes_accessed=cells * 30, transcendentals=0),
-    )(stats, *grads, *states, *prev)
-
-
-def place_kernel(w, lo, n, n_extra, own_u, own_d, got_u, got_d, *rest):
+    )(me, stats, *grads, *states, *prev)
+
+
+def place_kernel(w, lo, n, n_extra, got_u, got_d, *rest):
     out_u, out_d, buf_u, buf_d, sem_in, sem_out = rest[n_extra:]
-    d = lax.axis_index('data')
-    loads, stores = [], []
-    for k, (src_u, src_d) in enumerate(((own_u, own_d), (got_u, got_d))):
-        q = d if k == 0 else 1 - d
-        loads.append(pltpu.make_async_copy(src_u, buf_u.at[k], sem_in.at[k, 0]))
-        loads.append(pltpu.make_async_copy(src_d, buf_d.at[k], sem_in.at[k, 1]))
-        for i in range(n):
-            t = i + lo
-            cols = pl.ds(((t % 2) * NB + t // 2) * HB, HB)
-            stores.append((2 * k, pltpu.make_async_copy(
-                buf_u.at[k, i], out_u.at[w, pl.ds(pl.multiple_of(q * (D // 2), 8), D // 2), cols], sem_out.at[k, i])))
-            rows = pl.ds(pl.multiple_of(q * (FF // 2) + t * 128, 8), 128)
-            stores.append((2 * k + 1, pltpu.make_async_copy(buf_d.at[k, i], out_d.at[w, rows, :], sem_out.at[k, n + i])))
+    q = 1 - lax.axis_index('data')
+    loads = [pltpu.make_async_copy(got_u, buf_u, sem_in.at[0]), pltpu.make_async_copy(got_d, buf_d, sem_in.at[1])]
+    stores = []
+    for i in range(n):
+        t = i + lo
+        cols = pl.ds(((t % 2) * NB + t // 2) * HB, HB)
+        stores.append((0, pltpu.make_async_copy(
+            buf_u.at[i], out_u.at[w, pl.ds(pl.multiple_of(q * (D // 2), 8), D // 2), cols], sem_out.at[i])))
+        rows = pl.ds(pl.multiple_of(q * (FF // 2) + t * 128, 8), 128)
+        stores.append((1, pltpu.make_async_copy(buf_d.at[i], out_d.at[w, rows, :], sem_out.at[n + i])))
     for c in loads:
         c.start()
     for k, c in enumerate(loads):
@@ -481,22 +519,22 @@
         st.wait()
 
 
-def place(w, lo, own, got, prev, after):
-    n = own[0].shape[0]
+def place(w, lo, got, weights, after):
+    n = got[0].shape[0]
     any_spec = pl.BlockSpec(memory_space=pl.ANY)
-    extra = list(prev) + list(after)
-    cells = 2 * n * (D // 2 * HB + 128 * D)
+    extra = list(weights) + list(after)
+    cells = n * (D // 2 * HB + 128 * D)
     return pl.pallas_call(
         lambda *refs: place_kernel(w, lo, n, len(extra), *refs),
         out_shape=(jax.ShapeDtypeStruct((2, D, FF), BF16), jax.ShapeDtypeStruct((2, FF, D), BF16)),
-        in_specs=[any_spec] * (4 + len(extra)),
+        in_specs=[any_spec] * (2 + len(extra)),
         out_specs=(any_spec, any_spec),
-        scratch_shapes=[pltpu.VMEM((2, n, D // 2, HB), BF16), pltpu.VMEM((2, n, 128, D), BF16),
-                        pltpu.SemaphoreType.DMA((2, 2)), pltpu.SemaphoreType.DMA((2, 2 * n))],
-        input_output_aliases={4 + k: k for k in range(len(prev))},
+        scratch_shapes=[pltpu.VMEM((n, D // 2, HB), BF16), pltpu.VMEM((n, 128, D), BF16),
+                        pltpu.SemaphoreType.DMA((2,)), pltpu.SemaphoreType.DMA((2 * n,))],
+        input_output_aliases={2 + k: k for k in range(2)},
         compiler_params=pltpu.CompilerParams(vmem_limit_bytes=67043328),
         cost_estimate=pl.CostEstimate(flops=cells * 100, bytes_accessed=cells * 4, transcendentals=0),
-    )(*own, *got, *extra)
+    )(*got, *extra)
 
 
 def swap(halves):
@@ -512,9 +550,7 @@
     both_axes = [(r * 2 + d, (r ^ 3) * 2 + d) for r in range(4) for d in range(2)]
 
     def device_step(inp_rows, out_grad, w_up, w_down, master_up, master_down, mom_up, mom_down, var_up, var_down, clip_norm):
-        pre_one = jnp.dot(inp_rows, w_up[0], preferred_element_type=F32).astype(BF16)
-        act_one = gelu_value(pre_one.astype(F32)).astype(BF16)
-        mid_rows = jnp.dot(act_one, w_down[0], preferred_element_type=F32).astype(BF16)
+        pre_one, mid_rows = forward(inp_rows, w_up, w_down)
         g_up, g_down, g_tail, stats = backward_reduce(clip_norm.reshape(1), mid_rows, out_grad, inp_rows, pre_one, w_up, w_down)
         axes = ('replica', 'data')
         tails = [g_tail]
@@ -522,19 +558,17 @@
             tails.append(lax.ppermute(g_tail, axes, perm))
         states = [master_up, mom_up, var_up, master_down, mom_down, var_down]
         cut = 2 * (NB - TAIL)
-        *new, wu, wd = adam(stats, [g_up, g_down], states, [], 1, 0, 2 * NB)
-        own_a = [wu, wd]
-        got_a = swap(own_a)
-        *new, wu, wd = adam(stats, [g_up, g_down], states, new, 0, 0, cut)
-        own_b = [wu, wd]
-        got_b = swap(own_b)
-        weights = place(1, 0, own_a, got_a, [], [wu])
-        *new, wu, wd = adam(stats, tails, states, new, 0, cut, 2 * NB, tail=True)
-        own_c = [wu, wd]
-        got_c = swap(own_c)
-        weights = place(0, 0, own_b, got_b, weights, [wu])
-        weights = place(0, cut, own_c, got_c, weights, [])
-        m_up, o_up, v_up, m_down, o_down, v_down = new
-        return (weights[0], weights[1], m_up, m_down, o_up, o_down, v_up, v_down, stats[0, 0, 0])
+        me = lax.axis_index('data').astype(jnp.int32).reshape(1)
+        *new, wu, wd = adam(me, stats, [g_up, g_down], states, [], 1, 0, 2 * NB)
+        got_a = swap([wu, wd])
+        *new, wu, wd = adam(me, stats, [g_up, g_down], states, new, 0, 0, cut)
+        got_b = swap([wu, wd])
+        new[6:] = place(1, 0, got_a, new[6:], [])
+        *new, wu, wd = adam(me, stats, tails, states, new, 0, cut, 2 * NB, tail=True)
+        got_c = swap([wu, wd])
+        new[6:] = place(0, 0, got_b, new[6:], [])
+        new[6:] = place(0, cut, got_c, new[6:], [])
+        m_up, o_up, v_up, m_down, o_down, v_down, new_up, new_down = new
+        return (new_up, new_down, m_up, m_down, o_up, o_down, v_up, v_down, stats[0, 0, 0])
 
     return jax.shard_map(device_step, mesh=mesh, in_specs=(batch_spec, batch_spec, whole_spec, whole_spec, shard_spec, shard_spec, shard_spec, shard_spec, shard_spec, shard_spec, whole_spec), out_specs=(whole_spec, whole_spec, shard_spec, shard_spec, shard_spec, shard_spec, shard_spec, shard_spec, whole_spec), check_vma=False)

time: 485 us -> 465 us (0.959)
  matrix products: 56.9 us -> 0 us
  Pallas kernels: 384 us -> 426 us
    dot_general x2 -> x0, matrix products: 56.9 us -> none  [the longest x1 29.9 us: device_step(): jnp.dot(act_one, w_down[0], preferred_element_type=F32).astype(BF16)]
    pallas_call x3 -> x4, Pallas kernels: 55.2 us -> 103 us  [the longest x3 57.6 us: adam(): pl.pallas_call(lambda *refs: adam_body(tail, len(prev), *refs), out_shape...]
    pallas_call x3, Pallas kernels: 15.9 us -> 9.6 us  [place(): pl.pallas_call(lambda *refs: place_kernel(w, lo, n, len(extra), *refs), o...]
    ppermute x3, waiting for transfers between devices: 36.4 us -> 31.2 us  [device_step(): tails.append(lax.ppermute(g_tail, axes, perm))]
  transfers between devices with their start and end apart: 9 -> 9, of which waited for: 1 -> 2; matrix products, arithmetic and copies ran while one was open for 0% -> 0% of each run, Pallas kernels for 8% -> 8%
where the time goes in v2:
time: 465 us
  Pallas kernels  426 us (92%)
  waiting for transfers between devices  31.6 us (7%)
  starting transfers between devices  5.05 us (1%)
    pallas_call x1, Pallas kernels, backward_reduce(): pl.pallas_call(mega_kernel, out_shape=(jax.ShapeDtypeStruct((2, NB, D //...  313 us
    pallas_call x3, Pallas kernels, adam(): pl.pallas_call(lambda *refs: adam_body(tail, len(prev), *refs), out_shape...  57.6 us
    pallas_call x1, Pallas kernels, forward(): pl.pallas_call(forward_body, grid=(B // rows,), out_shape=(jax.ShapeDtype...  45.9 us
    ppermute x3, waiting for transfers between devices, device_step(): tails.append(lax.ppermute(g_tail, axes, perm))  31.2 us
    pallas_call x3, Pallas kernels, place(): pl.pallas_call(lambda *refs: place_kernel(w, lo, n, len(extra), *refs), o...  9.6 us
  transfers between devices with their start and end apart: 9, of which 2 were waited for; matrix products, arithmetic and copies ran while one was open for 0% of the time, Pallas kernels for 8%

profile of v2, /device:TPU:0, one launch (start us, length us, event | category | flops | bytes accessed | tf_op | source)
XLA Modules:
  0.0 465.0 jit_solution(54684405374719143)
XLA Ops:
  1.3 45.9 %forward.1 = (bf16[4096,3072]{1,0:T(8,128)(2,1)}, bf16[4096,768]{1,0:T(8,128)(2,1)}) custom-call(bf16[4096,768]{1,0:T(8,128)(2,1)} %x_hbm.1, bf16[2,768,3072]{2,1,0:T(8,128)(2,1)} %wu_hbm.1, bf16[2,3072,768]{2,1,0:T(8,128)(2,1)} %wd_hbm.1), custom_call_target="tpu_custom_call" | custom-call | tf_op jit(solution)/shard_map/forward/pallas_call | solution.py:401
  47.2 312.5 %backward_reduce.1 = (f32[2,6,384,512]{3,2,1,0:T(8,128)}, f32[2,1536,768]{2,1,0:T(8,128)}, f32[3,2,192,256]{3,2,1,0:T(8,128)}, f32[2,8,128]{2,1,0:T(8,128)}) custom-call(f32[1]{0:T(128)} %bitcast.3.clip_ref, bf16[4096,768]{1,0:T(8,128)(2,1)} %get-tuple-element.51.h_hbm, bf16[4096,768]{1,0:T(8,128)(2,1)} %dy_hbm.1, bf16[4096,768]{1,0:T(8,128)(2,1)} %x_hbm.1, ...), custom_call_target="tpu_custom_call" | custom-call | tf_op jit(solution)/shard_map/backward_reduce/pallas_call | solution.py:372
  359.7 27.6 %shard_map.178 = (f32[2,384,3072]{2,1,0:T(8,128)}, f32[2,384,3072]{2,1,0:T(8,128)}, f32[2,384,3072]{2,1,0:T(8,128)}, f32[2,1536,768]{2,1,0:T(8,128)}, f32[2,1536...) custom-call(s32[1]{0:T(128)} %bitcast.refs_0_, ...), custom_call_target="tpu_custom_call" | custom-call | flops 943718400 | bytes 70778880 | tf_op jit(solution)/shard_map/pallas_call | solution.py:482
  387.3 0.0 collective-permute-start.3
  387.4 0.5 collective-permute-start.4
  387.9 0.2 collective-permute-start
  388.1 1.9 collective-permute-start.1
  390.0 1.4 collective-permute-start.2
  391.4 14.4 %shard_map.179 = (f32[2,384,3072]{2,1,0:T(8,128)}, f32[2,384,3072]{2,1,0:T(8,128)}, f32[2,384,3072]{2,1,0:T(8,128)}, f32[2,1536,768]{2,1,0:T(8,128)}, f32[2,1536...) custom-call(s32[1]{0:T(128)} %bitcast.refs_0_, ...), custom_call_target="tpu_custom_call", output_to_operand_aliasing={{0}: (10, {}), {1}: (11, {}), {2}: (12, {}), {3}: (13, {}),... | custom-call | flops 471859200 | bytes 35389440 | tf_op jit(solution)/shard_map/pallas_call | solution.py:482
  405.7 0.0 collective-permute-done.3.refs_0_
  405.7 0.0 collective-permute-start.7
  405.8 0.0 collective-permute-done.4.refs_1_
  405.8 0.5 collective-permute-start.8
  406.3 4.0 shard_map.180
  410.3 31.2 %collective-permute-done.refs_3_ = f32[3,2,192,256]{3,2,1,0:T(8,128)} collective-permute-done((f32[3,2,192,256]{3,2,1,0:T(8,128)}, f32[3,2,192,256]{3,2,1,0:T(8,128)}, u32[]{:S(2)}, u32[]{:S(2)}) %collective-permute-start) | collective-permute-done | bytes 1179680 | tf_op jit(solution)/shard_map/ppermute | solution.py:558
  441.5 0.0 collective-permute-done.1.refs_4_
  441.5 0.0 collective-permute-done.2.refs_5_
  441.5 15.6 %shard_map.181 = (f32[2,384,3072]{2,1,0:T(8,128)}, f32[2,384,3072]{2,1,0:T(8,128)}, f32[2,384,3072]{2,1,0:T(8,128)}, f32[2,1536,768]{2,1,0:T(8,128)}, f32[2,1536...) custom-call(s32[1]{0:T(128)} %bitcast.refs_0_, ...), custom_call_target="tpu_custom_call", output_to_operand_aliasing={{0}: (12, {}), {1}: (13, {}), {2}: (14, {}), {3}: (15, {}),... | custom-call | flops 471859200 | bytes 35389440 | tf_op jit(solution)/shard_map/pallas_call | solution.py:482
  457.1 0.0 collective-permute-start.5
  457.2 0.5 collective-permute-start.6
  457.7 1.2 slice.3
  458.9 0.0 collective-permute-done.7.refs_0_
  458.9 0.0 collective-permute-done.8.refs_1_
  458.9 2.8 shard_map.182
  461.7 0.0 collective-permute-done.5.refs_0_
  461.7 0.4 collective-permute-done.6.refs_1_
  462.0 2.8 shard_map.183
Async XLA Ops:
  387.3 18.4 %collective-permute-start.3 = (bf16[12,384,256]{2,1,0:T(8,128)(2,1)}, bf16[12,384,256]{2,1,0:T(8,128)(2,1)}, u32[]{:S(2)}, u32[]{:S(2)}) collective-permute-start(bf16[12,384,256]{2,1,0:T(8,128)(2,1)} %get-tuple-element.71), channel_id=1, source_target_pairs={{0,1},{1,0},{2,3},{3,2},{4,5},{5,4},{6,7},{7,6}} | collective-permute-start | bytes 7077896 | tf_op jit(solution)/shard_map/ppermute | solution.py:541
  387.4 18.4 %collective-permute-start.4 = (bf16[12,128,768]{2,1,0:T(8,128)(2,1)}, bf16[12,128,768]{2,1,0:T(8,128)(2,1)}, u32[]{:S(2)}, u32[]{:S(2)}) collective-permute-start(bf16[12,128,768]{2,1,0:T(8,128)(2,1)} %get-tuple-element.72), channel_id=1, source_target_pairs={{0,1},{1,0},{2,3},{3,2},{4,5},{5,4},{6,7},{7,6}} | collective-permute-start | bytes 7077896 | tf_op jit(solution)/shard_map/ppermute | solution.py:541
  387.9 53.6 %collective-permute-start = (f32[3,2,192,256]{3,2,1,0:T(8,128)}, f32[3,2,192,256]{3,2,1,0:T(8,128)}, u32[]{:S(2)}, u32[]{:S(2)}) collective-permute-start(f32[3,2,192,256]{3,2,1,0:T(8,128)} %get-tuple-element.54.refs_2_), channel_id=1, source_target_pairs={{0,4},{1,3},{2,6},{3,1},{4,0},{5,7},{6,2},{7,5}} | collective-permute-start | bytes 3538952 | tf_op jit(solution)/shard_map/ppermute | solution.py:558
  388.1 53.4 %collective-permute-start.1 = (f32[3,2,192,256]{3,2,1,0:T(8,128)}, f32[3,2,192,256]{3,2,1,0:T(8,128)}, u32[]{:S(2)}, u32[]{:S(2)}) collective-permute-start(f32[3,2,192,256]{3,2,1,0:T(8,128)} %get-tuple-element.54.refs_2_), channel_id=1, source_target_pairs={{0,2},{1,5},{2,0},{3,7},{4,6},{5,1},{6,4},{7,3}} | collective-permute-start | bytes 3538952 | tf_op jit(solution)/shard_map/ppermute | solution.py:558
  390.0 51.5 %collective-permute-start.2 = (f32[3,2,192,256]{3,2,1,0:T(8,128)}, f32[3,2,192,256]{3,2,1,0:T(8,128)}, u32[]{:S(2)}, u32[]{:S(2)}) collective-permute-start(f32[3,2,192,256]{3,2,1,0:T(8,128)} %get-tuple-element.54.refs_2_), channel_id=1, source_target_pairs={{0,6},{1,7},{2,4},{3,5},{4,2},{5,3},{6,0},{7,1}} | collective-permute-start | bytes 3538952 | tf_op jit(solution)/shard_map/ppermute | solution.py:558
  405.7 53.1 %collective-permute-start.7 = (bf16[6,384,256]{2,1,0:T(8,128)(2,1)}, bf16[6,384,256]{2,1,0:T(8,128)(2,1)}, u32[]{:S(2)}, u32[]{:S(2)}) collective-permute-start(bf16[6,384,256]{2,1,0:T(8,128)(2,1)} %get-tuple-element.79), channel_id=1, source_target_pairs={{0,1},{1,0},{2,3},{3,2},{4,5},{5,4},{6,7},{7,6}} | collective-permute-start | bytes 3538952 | tf_op jit(solution)/shard_map/ppermute | solution.py:541
  405.8 53.1 %collective-permute-start.8 = (bf16[6,128,768]{2,1,0:T(8,128)(2,1)}, bf16[6,128,768]{2,1,0:T(8,128)(2,1)}, u32[]{:S(2)}, u32[]{:S(2)}) collective-permute-start(bf16[6,128,768]{2,1,0:T(8,128)(2,1)} %get-tuple-element.80), channel_id=1, source_target_pairs={{0,1},{1,0},{2,3},{3,2},{4,5},{5,4},{6,7},{7,6}} | collective-permute-start | bytes 3538952 | tf_op jit(solution)/shard_map/ppermute | solution.py:541
  457.1 4.5 collective-permute-start.5
  457.2 4.9 %collective-permute-start.6 = (bf16[6,128,768]{2,1,0:T(8,128)(2,1)}, bf16[6,128,768]{2,1,0:T(8,128)(2,1)}, u32[]{:S(2)}, u32[]{:S(2)}) collective-permute-start(bf16[6,128,768]{2,1,0:T(8,128)(2,1)} %get-tuple-element.78), channel_id=1, source_target_pairs={{0,1},{1,0},{2,3},{3,2},{4,5},{5,4},{6,7},{7,6}} | collective-permute-start | bytes 3538952 | tf_op jit(solution)/shard_map/ppermute | solution.py:541

commit v3 on v2

--- a/solution.py
+++ b/solution.py
@@ -30,7 +30,7 @@
 FULL = STEPS - TAIL
 SQRT_HALF = 0.7071067811865476
 PDF_SCALE = 0.3989422804014327
-NBUF = 2
+NBUF = 4
 EXP_SCALE = -0.5 * 1.4426950408889634
 
 
@@ -198,18 +198,18 @@
             post(pit, pstage, pt)
 
     ssq[0] = jnp.zeros((8, 128), F32)
-    for i in range(NCH):
-        row_copy(h_hbm, abuf, asem, i).start()
-        row_copy(dy_hbm, bbuf, bsem, i).start()
-        if i == 0:
-            up, down = w_copies(0)
-            for c in up + down:
-                c.start()
+    up, down = w_copies(0)
+    for c in [row_copy(h_hbm, abuf, asem, 0)] + up + [row_copy(dy_hbm, bbuf, bsem, 0)] + down:
+        c.start()
 
     barrier = pltpu.get_barrier_semaphore()
-    for dev in (partner, n1, n2):
-        pl.semaphore_signal(barrier, inc=1, device_id=dev, device_id_type=MESH)
-    pl.semaphore_wait(barrier, 3)
+    for fy in range(2):
+        for fx in range(2):
+            for fd in range(2):
+                if fy + fx + fd:
+                    dev = (2 * (y + fy - 2 * fy * y) + x + fx - 2 * fx * x, d + fd - 2 * fd * d)
+                    pl.semaphore_signal(barrier, inc=1, device_id=dev, device_id_type=MESH)
+    pl.semaphore_wait(barrier, 7)
 
     def zero_c(i, carry):
         cbuf[rows_of(i * 128, 128), :] = jnp.zeros((128, D), F32)
@@ -235,6 +235,11 @@
             def _():
                 row_copy(h_hbm, abuf, asem, i).wait()
                 row_copy(dy_hbm, bbuf, bsem, i).wait()
+
+                @pl.when(i + 1 < NCH)
+                def _():
+                    row_copy(h_hbm, abuf, asem, i + 1).start()
+                    row_copy(dy_hbm, bbuf, bsem, i + 1).start()
 
             z = dot(abuf[rows, :], wa[slot], ((1,), (0,))).astype(BF16)
             zb[rows, :] = z
@@ -341,18 +346,26 @@
 
     lax.fori_loop(0, 4 * (STEPS + 1) + 2, quarter, 0)
 
-    for i, dev in enumerate((partner, (r + x_off, d), (r + y_off, d))):
-        c = pltpu.make_async_remote_copy(src_ref=ssq.at[i], dst_ref=sq_in.at[i], send_sem=nsend.at[i],
-                                         recv_sem=nrecv.at[i], device_id=dev, device_id_type=MESH)
+    peers = [(2 * (y + fy - 2 * fy * y) + x + fx - 2 * fx * x, d + fd - 2 * fd * d)
+             for fy in range(2) for fx in range(2) for fd in range(2)]
+    sq_in[0] = ssq[0]
+    for t in range(FULL, STEPS):
+        for it in (item_d, item_u):
+            for tc in tail_out(it, t):
+                tc.wait()
+    exchange = [pltpu.make_async_remote_copy(src_ref=ssq.at[0], dst_ref=sq_in.at[k], send_sem=nsend.at[k],
+                                             recv_sem=nrecv.at[k], device_id=peers[k], device_id_type=MESH)
+                for k in range(1, 8)]
+    for c in exchange:
         c.start()
-        if i == 0:
-            for t in range(FULL, STEPS):
-                for it in (item_d, item_u):
-                    for tc in tail_out(it, t):
-                        tc.wait()
+    for c in exchange:
         c.wait()
-        ssq[i + 1] = ssq[i] + sq_in[i]
-    total = jnp.sum(ssq[3], axis=0, keepdims=True)
+    total = jnp.zeros((8, 128), F32)
+    for iy in range(2):
+        for ix in range(2):
+            for dd in range(2):
+                total = total + sq_in[4 * lax.rem(iy + y, 2) + 2 * lax.rem(ix + x, 2) + lax.rem(dd + d, 2)]
+    total = jnp.sum(total, axis=0, keepdims=True)
     total = jnp.sum(total, axis=1, keepdims=True)
     norm = jnp.sqrt(total)
     scale = jnp.minimum(1.0, clip_ref[0] / (norm + NORM_EPS))
@@ -380,8 +393,8 @@
         scratch_shapes=[vmem((B, D), BF16), vmem((B, D), BF16), vmem((B, D), F32),
                         vmem((2, D, BF), BF16), vmem((2, BF, D), BF16), vmem((B, BF), BF16)]
         + item(HB, D, (BF, D)) + item(D // 2, BF, (D, BF))
-        + [vmem((4, 8, 128), F32), vmem((3, 8, 128), F32)]
-        + [dma((NCH,)), dma((NCH,)), dma((2, 4)), dma((NCH, 2)), dma((TAIL, 2, 3)), dma((3,)), dma((3,))]
+        + [vmem((1, 8, 128), F32), vmem((8, 8, 128), F32)]
+        + [dma((NCH,)), dma((NCH,)), dma((2, 4)), dma((NCH, 2)), dma((TAIL, 2, 3)), dma((8,)), dma((8,))]
         + [dma((5, SLOTS)), dma((5, SLOTS)), dma((SLOTS,))] * 2,
         compiler_params=pltpu.CompilerParams(collective_id=0, has_side_effects=True, vmem_limit_bytes=67043328),
         name='backward_reduce',
@@ -411,130 +424,197 @@
     )(x, w_up, w_down)
 
 
-def adam_rule(s, g, master_ref, mom_ref, var_ref, new_master_ref, new_mom_ref, new_var_ref, w_refs):
-    mom = BETA1 * mom_ref[0] + (1.0 - BETA1) * s * g
-    var = BETA2 * var_ref[0] + (1.0 - BETA2) * (s * s) * (g * g)
-    master = master_ref[0] - LEARN_RATE * (mom / BIAS_ONE) / (jnp.sqrt(var / BIAS_TWO) + ADAM_EPS)
-    new_mom_ref[0] = mom
-    new_var_ref[0] = var
-    new_master_ref[0] = master
-    w = master.astype(BF16)
-    for ref in w_refs:
-        ref[0] = w
-
-
-def adam_body(tail, n_alias, me, stats, *refs):
+def adam_rule(s, g, master, mom, var):
+    mom = BETA1 * mom + (1.0 - BETA1) * s * g
+    var = BETA2 * var + (1.0 - BETA2) * (s * s) * (g * g)
+    master = master - LEARN_RATE * (mom / BIAS_ONE) / (jnp.sqrt(var / BIAS_TWO) + ADAM_EPS)
+    return master, mom, var
+
+
+def adam_kernel(w, j0, nj, tail, n_alias, stats, *refs):
+    n = 2 * nj
+    ru = D // 2 // n
+    n_grads = 4 if tail else 2
+    grads, refs = refs[:n_grads], refs[n_grads:]
+    states, refs = refs[:6], refs[6 + n_alias:]
+    outs, refs = refs[:10], refs[10:]
+    if not n_alias:
+        norm_out, refs = refs[0], refs[1:]
+        norm_out[0] = jnp.max(stats[0])
+    in_u, in_d, g_u, g_d, out_u, out_d, w_u, w_d, gt, isem, osem, gsem = refs
+    d = lax.axis_index('data')
     s = stats[1, 0:1, 0:1]
+
+    def up_at(ref, p, row0, size):
+        return ref.at[w, pl.ds(pl.multiple_of(row0, 8), size), pl.ds((p * NB + j0) * HB, nj * HB)]
+
+    def loads(i):
+        k = lax.rem(i, NBUF)
+        row = pl.ds(pl.multiple_of((i + 2 * j0) * 128, 8), 128)
+        cs = []
+        if not tail:
+            rows = pl.ds(pl.multiple_of(i * ru, 8), ru)
+            cs.append(pltpu.make_async_copy(grads[0].at[w, pl.ds(j0, nj), rows, :], g_u.at[k], isem.at[k, 9]))
+            cs.append(pltpu.make_async_copy(grads[1].at[w, row, :], g_d.at[k], isem.at[k, 10]))
+        for q in range(3):
+            for p in range(2):
+                cs.append(pltpu.make_async_copy(up_at(states[q], p, i * ru, ru), in_u.at[k, q, p], isem.at[k, 2 * q + p]))
+            cs.append(pltpu.make_async_copy(states[3 + q].at[w, row, :], in_d.at[k, q], isem.at[k, 6 + q]))
+        return cs
+
+    def stores(i):
+        k = lax.rem(i, 2)
+        row = pl.ds(pl.multiple_of((i + 2 * j0) * 128, 8), 128)
+        cs = []
+        for q in range(3):
+            for p in range(2):
+                cs.append(pltpu.make_async_copy(out_u.at[k, q, p], up_at(outs[q], p, i * ru, ru), osem.at[k, 2 * q + p]))
+            cs.append(pltpu.make_async_copy(out_d.at[k, q], outs[3 + q].at[w, row, :], osem.at[k, 6 + q]))
+        for p in range(2):
+            cs.append(pltpu.make_async_copy(w_u.at[k, p], up_at(outs[6], p, d * (D // 2) + i * ru, ru), osem.at[k, 9 + p]))
+        my_down = pl.ds(pl.multiple_of(d * (FF // 2) + (i + 2 * j0) * 128, 8), 128)
+        cs.append(pltpu.make_async_copy(w_d.at[k], outs[7].at[w, my_down, :], osem.at[k, 11]))
+        cs.append(pltpu.make_async_copy(w_u.at[k], outs[8].at[:, pl.ds(pl.multiple_of(i * ru, 8), ru), :], osem.at[k, 12]))
+        cs.append(pltpu.make_async_copy(w_d.at[k], outs[9].at[i], osem.at[k, 13]))
+        return cs
+
+    for i in range(NBUF):
+        for c in loads(i):
+            c.start()
     if tail:
-        own, from_n2, from_n1, from_diag = refs[:4]
-        refs = refs[4:]
+        g_loads = [pltpu.make_async_copy(grads[q], gt.at[q], gsem.at[q]) for q in range(4)]
+        for c in g_loads:
+            c.start()
+        for c in g_loads:
+            c.wait()
         r = lax.axis_index('replica')
-        d = lax.axis_index('data')
         x, y = lax.rem(r, 2), lax.div(r, 2)
         a = (1 - d) * x + d * y
         b = (1 - d) * y + d * x
-        i = pl.program_id(0)
-        half = lax.rem(i, 2)
-
-        def pick(qa, qb, ty, rows):
-            da = lax.rem(qa + a, 2)
-            db = lax.rem(qb + b, 2)
-            near = jnp.where(db == 0, own[0, ty, rows, :], from_n2[0, ty, rows, :])
-            far = jnp.where(db == 0, from_n1[0, ty, rows, :], from_diag[0, ty, rows, :])
-            return jnp.where(da == 0, near, far)
-
-        up_rows = pl.ds(pl.multiple_of(half * 96, 8), 96)
-        g_up = jnp.concatenate([pick(q // 2, q % 2, 1, up_rows) for q in range(4)], axis=0)
-        g_down = jnp.concatenate([jnp.concatenate([pick(half, qb, 0, pl.ds(p * 64, 64)) for p in range(3)], axis=1)
-                                  for qb in range(2)], axis=0)
-    else:
-        g_up = refs[0][0, 0]
-        g_down = refs[1][0]
-        refs = refs[2:]
-    states, outs = refs[:6], refs[6 + n_alias:]
-    adam_rule(s, g_up, *states[:3], *outs[:3], (outs[6], outs[8]))
-    adam_rule(s, g_down, *states[3:], *outs[3:6], (outs[7], outs[9]))
-
-
-def adam(me, stats, grads, states, prev, w, lo, hi, tail=False):
+
+    def block(i, carry):
+        k = lax.rem(i, NBUF)
+        o = lax.rem(i, 2)
+        for c in loads(i):
+            c.wait()
+
+        @pl.when(i >= 2)
+        def _():
+            for c in stores(i - 2):
+                c.wait()
+
+        for t in range(ru // 32):
+            rows = slice(t * 32, (t + 1) * 32)
+            if tail:
+                third = i * (ru // 32) + t
+                quarter = lax.div(third, 3)
+                src = 2 * lax.rem(lax.div(quarter, 2) + a, 2) + lax.rem(lax.rem(quarter, 2) + b, 2)
+                g_row = lax.rem(third, 3) * 32
+            for p in range(2):
+                for j in range(nj):
+                    cols = slice(j * HB, (j + 1) * HB)
+                    if tail:
+                        g = gt[src, j, 1, pl.ds(pl.multiple_of(p * 96 + g_row, 8), 32), :]
+                    else:
+                        g = g_u[k, j, rows, p * HB:(p + 1) * HB]
+                    res = adam_rule(s, g, in_u[k, 0, p, rows, cols], in_u[k, 1, p, rows, cols], in_u[k, 2, p, rows, cols])
+                    for q in range(3):
+                        out_u[o, q, p, rows, cols] = res[q]
+                    w_u[o, p, rows, cols] = res[0].astype(BF16)
+        for t in range(8):
+            rows = slice(t * 16, (t + 1) * 16)
+            if tail:
+                half = lax.rem(i, 2)
+                src = 2 * lax.rem(half + a, 2) + lax.rem(t // 4 + b, 2)
+                g = jnp.concatenate([gt[src, lax.div(i, 2), 0, p * 64 + (t % 4) * 16:p * 64 + (t % 4) * 16 + 16, :] for p in range(3)], axis=1)
+            else:
+                g = g_d[k, rows, :]
+            res = adam_rule(s, g, in_d[k, 0, rows, :], in_d[k, 1, rows, :], in_d[k, 2, rows, :])
+            for q in range(3):
+                out_d[o, q, rows, :] = res[q]
+            w_d[o, rows, :] = res[0].astype(BF16)
+        for c in stores(i):
+            c.start()
+
+        @pl.when(i + NBUF < n)
+        def _():
+            for c in loads(i + NBUF):
+                c.start()
+
+        return carry
+
+    lax.fori_loop(0, n, block, 0)
+    for i in (n - 2, n - 1):
+        for c in stores(i):
+            c.wait()
+
+
+def adam(stats, grads, states, prev, w, j0, nj, tail=False):
     any_spec = pl.BlockSpec(memory_space=pl.ANY)
-    deep = pl.Buffered(NBUF)
-
-    def col(i):
-        return lax.rem(i + lo, 2) * NB + lax.div(i + lo, 2)
-
-    def specs(**kw):
-        up = pl.BlockSpec((1, D // 2, HB), lambda i, me: (w, 0, col(i)), **kw)
-        down = pl.BlockSpec((1, 128, D), lambda i, me: (w, i + lo, 0), **kw)
-        return [up] * 3 + [down] * 3
-
-    if tail:
-        g_specs = [pl.BlockSpec((1, 2, 192, 256), lambda i, me: (lax.div(i, 2), 0, 0, 0))] * 4
-    else:
-        g_specs = [pl.BlockSpec((1, 1, D // 2, HB), lambda i, me: (w, lax.div(i + lo, 2), 0, lax.rem(i + lo, 2)), pipeline_mode=deep),
-                   pl.BlockSpec((1, 128, D), lambda i, me: (w, i + lo, 0), pipeline_mode=deep)]
-    n = hi - lo
+    n = 2 * nj
+    ru = D // 2 // n
     full = [jax.ShapeDtypeStruct(v.shape, F32) for v in states]
     whole = [jax.ShapeDtypeStruct((2, D, FF), BF16), jax.ShapeDtypeStruct((2, FF, D), BF16)]
-    halves = [jax.ShapeDtypeStruct((n, D // 2, HB), BF16), jax.ShapeDtypeStruct((n, 128, D), BF16)]
-    first = 2 + len(grads) + 6
-    cells = n * (D // 2 * HB + 128 * D)
+    halves = [jax.ShapeDtypeStruct((2, D // 2, nj * HB), BF16), jax.ShapeDtypeStruct((n, 128, D), BF16)]
+    norm = [] if prev else [jax.ShapeDtypeStruct((1,), F32)]
+    first = 1 + len(grads) + 6
+    cells = D * nj * HB * 2
+    vmem, dma = pltpu.VMEM, pltpu.SemaphoreType.DMA
     return pl.pallas_call(
-        lambda *refs: adam_body(tail, len(prev), *refs),
-        out_shape=full + whole + halves,
-        grid_spec=pltpu.PrefetchScalarGridSpec(
-            num_scalar_prefetch=1,
-            grid=(n,),
-            in_specs=[pl.BlockSpec((2, 8, 128), lambda i, me: (0, 0, 0))] + g_specs + specs(pipeline_mode=deep) + [any_spec] * len(prev),
-            out_specs=specs() + [pl.BlockSpec((1, D // 2, HB), lambda i, me: (w, me[0], col(i))),
-                                 pl.BlockSpec((1, 128, D), lambda i, me: (w, me[0] * (FF // 256) + i + lo, 0)),
-                                 pl.BlockSpec((1, D // 2, HB), lambda i, me: (i, 0, 0)),
-                                 pl.BlockSpec((1, 128, D), lambda i, me: (i, 0, 0))]),
+        lambda *refs: adam_kernel(w, j0, nj, tail, len(prev), *refs),
+        out_shape=full + whole + halves + norm,
+        in_specs=[pl.BlockSpec(memory_space=pltpu.VMEM)] + [any_spec] * (len(grads) + 6 + len(prev)),
+        out_specs=[any_spec] * 10 + [pl.BlockSpec(memory_space=pltpu.SMEM)] * len(norm),
+        scratch_shapes=[vmem((NBUF, 3, 2, ru, nj * HB), F32), vmem((NBUF, 3, 128, D), F32),
+                        vmem((NBUF, nj, ru, BF), F32), vmem((NBUF, 128, D), F32),
+                        vmem((2, 3, 2, ru, nj * HB), F32), vmem((2, 3, 128, D), F32),
+                        vmem((2, 2, ru, nj * HB), BF16), vmem((2, 128, D), BF16),
+                        vmem((4, TAIL, 2, 192, 256), F32), dma((NBUF, 11)), dma((2, 14)), dma((4,))],
         input_output_aliases={first + k: k for k in range(len(prev))},
         compiler_params=pltpu.CompilerParams(vmem_limit_bytes=67043328),
         cost_estimate=pl.CostEstimate(flops=cells * 400, bytes_accessed=cells * 30, transcendentals=0),
-    )(me, stats, *grads, *states, *prev)
-
-
-def place_kernel(w, lo, n, n_extra, got_u, got_d, *rest):
-    out_u, out_d, buf_u, buf_d, sem_in, sem_out = rest[n_extra:]
+    )(stats, *grads, *states, *prev)
+
+
+def place_kernel(w, j0, nj, got_u, got_d, _u, _d, out_u, out_d, buf_u, buf_d, sem_in, sem_out):
     q = 1 - lax.axis_index('data')
-    loads = [pltpu.make_async_copy(got_u, buf_u, sem_in.at[0]), pltpu.make_async_copy(got_d, buf_d, sem_in.at[1])]
-    stores = []
-    for i in range(n):
-        t = i + lo
-        cols = pl.ds(((t % 2) * NB + t // 2) * HB, HB)
-        stores.append((0, pltpu.make_async_copy(
-            buf_u.at[i], out_u.at[w, pl.ds(pl.multiple_of(q * (D // 2), 8), D // 2), cols], sem_out.at[i])))
-        rows = pl.ds(pl.multiple_of(q * (FF // 2) + t * 128, 8), 128)
-        stores.append((1, pltpu.make_async_copy(buf_d.at[i], out_d.at[w, rows, :], sem_out.at[n + i])))
+    rows = pl.ds(pl.multiple_of(q * (D // 2), 8), D // 2)
+    loads, stores = [], []
+    for p in range(2):
+        loads.append(pltpu.make_async_copy(got_u.at[p], buf_u.at[p], sem_in.at[p]))
+        stores.append(pltpu.make_async_copy(buf_u.at[p], out_u.at[w, rows, pl.ds((p * NB + j0) * HB, nj * HB)], sem_out.at[p]))
+    for p in range(2):
+        part = pl.ds(p * nj, nj)
+        loads.append(pltpu.make_async_copy(got_d.at[part], buf_d.at[part], sem_in.at[2 + p]))
+        for i in range(nj):
+            t = p * nj + i
+            to = pl.ds(pl.multiple_of(q * (FF // 2) + (t + 2 * j0) * 128, 8), 128)
+            stores.append(pltpu.make_async_copy(buf_d.at[t], out_d.at[w, to, :], sem_out.at[2 + t]))
     for c in loads:
         c.start()
     for k, c in enumerate(loads):
         c.wait()
-        for kk, st in stores:
-            if kk == k:
-                st.start()
-    for kk, st in stores:
+        for st in stores[k:k + 1] if k < 2 else stores[2 + (k - 2) * nj:2 + (k - 1) * nj]:
+            st.start()
+    for st in stores:
         st.wait()
 
 
-def place(w, lo, got, weights, after):
-    n = got[0].shape[0]
+def place(w, j0, nj, got, weights):
     any_spec = pl.BlockSpec(memory_space=pl.ANY)
-    extra = list(weights) + list(after)
-    cells = n * (D // 2 * HB + 128 * D)
+    n = 2 * nj
+    cells = D * nj * HB * 2
     return pl.pallas_call(
-        lambda *refs: place_kernel(w, lo, n, len(extra), *refs),
+        lambda *refs: place_kernel(w, j0, nj, *refs),
         out_shape=(jax.ShapeDtypeStruct((2, D, FF), BF16), jax.ShapeDtypeStruct((2, FF, D), BF16)),
-        in_specs=[any_spec] * (2 + len(extra)),
+        in_specs=[any_spec] * 4,
         out_specs=(any_spec, any_spec),
-        scratch_shapes=[pltpu.VMEM((n, D // 2, HB), BF16), pltpu.VMEM((n, 128, D), BF16),
-                        pltpu.SemaphoreType.DMA((2,)), pltpu.SemaphoreType.DMA((2 * n,))],
+        scratch_shapes=[pltpu.VMEM((2, D // 2, nj * HB), BF16), pltpu.VMEM((n, 128, D), BF16),
+                        pltpu.SemaphoreType.DMA((4,)), pltpu.SemaphoreType.DMA((2 + n,))],
         input_output_aliases={2 + k: k for k in range(2)},
         compiler_params=pltpu.CompilerParams(vmem_limit_bytes=67043328),
         cost_estimate=pl.CostEstimate(flops=cells * 100, bytes_accessed=cells * 4, transcendentals=0),
-    )(*got, *extra)
+    )(*got, *weights)
 
 
 def swap(halves):
@@ -547,28 +627,27 @@
     shard_spec = P(None, 'data', None)
     first_axis = [(r * 2 + d, (r ^ (1 if d == 0 else 2)) * 2 + d) for r in range(4) for d in range(2)]
     second_axis = [(r * 2 + d, (r ^ (2 if d == 0 else 1)) * 2 + d) for r in range(4) for d in range(2)]
-    both_axes = [(r * 2 + d, (r ^ 3) * 2 + d) for r in range(4) for d in range(2)]
 
     def device_step(inp_rows, out_grad, w_up, w_down, master_up, master_down, mom_up, mom_down, var_up, var_down, clip_norm):
         pre_one, mid_rows = forward(inp_rows, w_up, w_down)
         g_up, g_down, g_tail, stats = backward_reduce(clip_norm.reshape(1), mid_rows, out_grad, inp_rows, pre_one, w_up, w_down)
         axes = ('replica', 'data')
         tails = [g_tail]
-        for perm in (second_axis, first_axis, both_axes):
+        for perm in (second_axis, first_axis):
             tails.append(lax.ppermute(g_tail, axes, perm))
+        tails.append(lax.ppermute(tails[1], axes, first_axis))
         states = [master_up, mom_up, var_up, master_down, mom_down, var_down]
-        cut = 2 * (NB - TAIL)
-        me = lax.axis_index('data').astype(jnp.int32).reshape(1)
-        *new, wu, wd = adam(me, stats, [g_up, g_down], states, [], 1, 0, 2 * NB)
+        cut = NB - TAIL
+        *new, wu, wd, norm = adam(stats, [g_up, g_down], states, [], 1, 0, NB)
         got_a = swap([wu, wd])
-        *new, wu, wd = adam(me, stats, [g_up, g_down], states, new, 0, 0, cut)
+        *new, wu, wd = adam(stats, [g_up, g_down], states, new, 0, 0, cut)
         got_b = swap([wu, wd])
-        new[6:] = place(1, 0, got_a, new[6:], [])
-        *new, wu, wd = adam(me, stats, tails, states, new, 0, cut, 2 * NB, tail=True)
+        new[6:] = place(1, 0, NB, got_a, new[6:])
+        *new, wu, wd = adam(stats, tails, states, new, 0, cut, TAIL, tail=True)
         got_c = swap([wu, wd])
-        new[6:] = place(0, 0, got_b, new[6:], [])
-        new[6:] = place(0, cut, got_c, new[6:], [])
+        new[6:] = place(0, 0, cut, got_b, new[6:])
+        new[6:] = place(0, cut, TAIL, got_c, new[6:])
         m_up, o_up, v_up, m_down, o_down, v_down, new_up, new_down = new
-        return (new_up, new_down, m_up, m_down, o_up, o_down, v_up, v_down, stats[0, 0, 0])
+        return (new_up, new_down, m_up, m_down, o_up, o_down, v_up, v_down, norm.reshape(()))
 
     return jax.shard_map(device_step, mesh=mesh, in_specs=(batch_spec, batch_spec, whole_spec, whole_spec, shard_spec, shard_spec, shard_spec, shard_spec, shard_spec, shard_spec, whole_spec), out_specs=(whole_spec, whole_spec, shard_spec, shard_spec, shard_spec, shard_spec, shard_spec, shard_spec, whole_spec), check_vma=False)

time: 465 us -> 455 us (0.978)
  Pallas kernels: 426 us -> 420 us
    ppermute x3 -> x2, waiting for transfers between devices: 31.2 us -> 26.8 us  [device_step(): tails.append(lax.ppermute(g_tail, axes, perm))]
  transfers between devices with their start and end apart: 9 -> 9, of which waited for: 2 -> 3; matrix products, arithmetic and copies ran while one was open for 0% -> 0% of each run, Pallas kernels for 8% -> 8%
where the time goes in v3:
time: 455 us; the launch traced here: 454 us
  Pallas kernels  420 us (92%)
  waiting for transfers between devices  28.6 us (6%)
    pallas_call x1, Pallas kernels, backward_reduce(): pl.pallas_call(mega_kernel, out_shape=(jax.ShapeDtypeStruct((2, NB, D //...  309 us
    pallas_call x3, Pallas kernels, adam(): pl.pallas_call(lambda *refs: adam_kernel(w, j0, nj, tail, len(prev), *ref...  55.7 us
    pallas_call x1, Pallas kernels, forward(): pl.pallas_call(forward_body, grid=(B // rows,), out_shape=(jax.ShapeDtype...  45.9 us
    ppermute x2, waiting for transfers between devices, device_step(): tails.append(lax.ppermute(g_tail, axes, perm))  26.8 us
  transfers between devices with their start and end apart: 9, of which 3 were waited for; matrix products, arithmetic and copies ran while one was open for 0% of the time, Pallas kernels for 8%

profile of v3, /device:TPU:0, one launch (start us, length us, event | category | flops | bytes accessed | tf_op | source)
XLA Modules:
  0.0 454.4 jit_solution(13293451192343950198)
XLA Ops:
  1.3 45.9 %forward.1 = (bf16[4096,3072]{1,0:T(8,128)(2,1)}, bf16[4096,768]{1,0:T(8,128)(2,1)}) custom-call(bf16[4096,768]{1,0:T(8,128)(2,1)} %x_hbm.1, bf16[2,768,3072]{2,1,0:T(8,128)(2,1)} %wu_hbm.1, bf16[2,3072,768]{2,1,0:T(8,128)(2,1)} %wd_hbm.1), custom_call_target="tpu_custom_call" | custom-call | tf_op jit(solution)/shard_map/forward/pallas_call | solution.py:414
  47.2 309.5 %backward_reduce.1 = (f32[2,6,384,512]{3,2,1,0:T(8,128)}, f32[2,1536,768]{2,1,0:T(8,128)}, f32[3,2,192,256]{3,2,1,0:T(8,128)}, f32[2,8,128]{2,1,0:T(8,128)}) custom-call(f32[1]{0:T(128)} %bitcast.2.clip_ref, bf16[4096,768]{1,0:T(8,128)(2,1)} %get-tuple-element.52.h_hbm, bf16[4096,768]{1,0:T(8,128)(2,1)} %dy_hbm.1, bf16[4096,768]{1,0:T(8,128)(2,1)} %x_hbm.1, ...), custom_call_target="tpu_custom_call" | custom-call | tf_op jit(solution)/shard_map/backward_reduce/pallas_call | solution.py:385
  356.7 26.4 %shard_map.178 = (f32[2,384,3072]{2,1,0:T(8,128)}, f32[2,384,3072]{2,1,0:T(8,128)}, f32[2,384,3072]{2,1,0:T(8,128)}, f32[2,1536,768]{2,1,0:T(8,128)}, f32[2,1536...) custom-call(f32[2,8,128]{2,1,0:T(8,128)} %get-tuple-element.54.refs_, ...), custom_call_target="tpu_custom_call" | custom-call | flops 943718400 | bytes 70778880 | tf_op jit(solution)/shard_map/pallas_call | solution.py:563
  383.1 0.1 collective-permute-start.3
  383.2 0.4 collective-permute-start.4
  383.6 0.6 collective-permute-start
  384.2 1.2 collective-permute-start.1
  385.4 26.8 %collective-permute-done.refs_2_ = f32[3,2,192,256]{3,2,1,0:T(8,128)} collective-permute-done((f32[3,2,192,256]{3,2,1,0:T(8,128)}, f32[3,2,192,256]{3,2,1,0:T(8,128)}, u32[]{:S(2)}, u32[]{:S(2)}) %collective-permute-start) | collective-permute-done | bytes 1179680 | tf_op jit(solution)/shard_map/ppermute | solution.py:637
  412.2 0.8 collective-permute-start.2
  413.0 14.1 %shard_map.179 = (f32[2,384,3072]{2,1,0:T(8,128)}, f32[2,384,3072]{2,1,0:T(8,128)}, f32[2,384,3072]{2,1,0:T(8,128)}, f32[2,1536,768]{2,1,0:T(8,128)}, f32[2,1536...) custom-call(f32[2,8,128]{2,1,0:T(8,128)} %get-tuple-element.54.refs_, ...), custom_call_target="tpu_custom_call", output_to_operand_aliasing={{0}: (9, {}), {1}: (10, {}), {2}: (11, {}), {3}: (12, {}), ... | custom-call | flops 471859200 | bytes 35389440 | tf_op jit(solution)/shard_map/pallas_call | solution.py:563
  427.2 0.0 collective-permute-start.7
  427.2 0.0 collective-permute-done.3.refs_0_
  427.2 0.5 collective-permute-start.8
  427.7 0.0 collective-permute-done.4.refs_1_
  427.7 3.8 shard_map.180
  431.5 0.0 collective-permute-done.1.refs_3_
  431.5 0.0 collective-permute-done.2.refs_4_
  431.6 15.2 %shard_map.181 = (f32[2,384,3072]{2,1,0:T(8,128)}, f32[2,384,3072]{2,1,0:T(8,128)}, f32[2,384,3072]{2,1,0:T(8,128)}, f32[2,1536,768]{2,1,0:T(8,128)}, f32[2,1536...) custom-call(f32[2,8,128]{2,1,0:T(8,128)} %get-tuple-element.54.refs_, ...), custom_call_target="tpu_custom_call", output_to_operand_aliasing={{0}: (11, {}), {1}: (12, {}), {2}: (13, {}), {3}: (14, {}),... | custom-call | flops 471859200 | bytes 35389440 | tf_op jit(solution)/shard_map/pallas_call | solution.py:563
  446.8 0.1 collective-permute-start.5
  446.8 0.5 collective-permute-start.6
  447.3 0.0 collective-permute-done.7.refs_0_
  447.3 0.0 collective-permute-done.8.refs_1_
  447.3 2.6 shard_map.182
  449.9 0.1 collective-permute-done.5.refs_0_
  450.0 1.7 collective-permute-done.6.refs_1_
  451.7 2.6 shard_map.183
Async XLA Ops:
  383.1 44.1 %collective-permute-start.3 = (bf16[2,384,1536]{2,1,0:T(8,128)(2,1)}, bf16[2,384,1536]{2,1,0:T(8,128)(2,1)}, u32[]{:S(2)}, u32[]{:S(2)}) collective-permute-start(bf16[2,384,1536]{2,1,0:T(8,128)(2,1)} %get-tuple-element.72), channel_id=1, source_target_pairs={{0,1},{1,0},{2,3},{3,2},{4,5},{5,4},{6,7},{7,6}} | collective-permute-start | bytes 7077896 | tf_op jit(solution)/shard_map/ppermute | solution.py:621
  383.2 44.5 %collective-permute-start.4 = (bf16[12,128,768]{2,1,0:T(8,128)(2,1)}, bf16[12,128,768]{2,1,0:T(8,128)(2,1)}, u32[]{:S(2)}, u32[]{:S(2)}) collective-permute-start(bf16[12,128,768]{2,1,0:T(8,128)(2,1)} %get-tuple-element.73), channel_id=1, source_target_pairs={{0,1},{1,0},{2,3},{3,2},{4,5},{5,4},{6,7},{7,6}} | collective-permute-start | bytes 7077896 | tf_op jit(solution)/shard_map/ppermute | solution.py:621
  383.6 28.6 %collective-permute-start = (f32[3,2,192,256]{3,2,1,0:T(8,128)}, f32[3,2,192,256]{3,2,1,0:T(8,128)}, u32[]{:S(2)}, u32[]{:S(2)}) collective-permute-start(f32[3,2,192,256]{3,2,1,0:T(8,128)} %get-tuple-element.55.refs_1_), channel_id=1, source_target_pairs={{0,4},{1,3},{2,6},{3,1},{4,0},{5,7},{6,2},{7,5}} | collective-permute-start | bytes 3538952 | tf_op jit(solution)/shard_map/ppermute | solution.py:637
  384.2 47.3 %collective-permute-start.1 = (f32[3,2,192,256]{3,2,1,0:T(8,128)}, f32[3,2,192,256]{3,2,1,0:T(8,128)}, u32[]{:S(2)}, u32[]{:S(2)}) collective-permute-start(f32[3,2,192,256]{3,2,1,0:T(8,128)} %get-tuple-element.55.refs_1_), channel_id=1, source_target_pairs={{0,2},{1,5},{2,0},{3,7},{4,6},{5,1},{6,4},{7,3}} | collective-permute-start | bytes 3538952 | tf_op jit(solution)/shard_map/ppermute | solution.py:637
  412.2 19.3 %collective-permute-start.2 = (f32[3,2,192,256]{3,2,1,0:T(8,128)}, f32[3,2,192,256]{3,2,1,0:T(8,128)}, u32[]{:S(2)}, u32[]{:S(2)}) collective-permute-start(f32[3,2,192,256]{3,2,1,0:T(8,128)} %collective-permute-done.refs_2_), channel_id=1, source_target_pairs={{0,2},{1,5},{2,0},{3,7},{4,6},{5,1},{6,4},{7,3}} | collective-permute-start | bytes 3538952 | tf_op jit(solution)/shard_map/ppermute | solution.py:638
  427.2 20.1 %collective-permute-start.7 = (bf16[2,384,768]{2,1,0:T(8,128)(2,1)}, bf16[2,384,768]{2,1,0:T(8,128)(2,1)}, u32[]{:S(2)}, u32[]{:S(2)}) collective-permute-start(bf16[2,384,768]{2,1,0:T(8,128)(2,1)} %get-tuple-element.80), channel_id=1, source_target_pairs={{0,1},{1,0},{2,3},{3,2},{4,5},{5,4},{6,7},{7,6}} | collective-permute-start | bytes 3538952 | tf_op jit(solution)/shard_map/ppermute | solution.py:621
  427.2 20.1 %collective-permute-start.8 = (bf16[6,128,768]{2,1,0:T(8,128)(2,1)}, bf16[6,128,768]{2,1,0:T(8,128)(2,1)}, u32[]{:S(2)}, u32[]{:S(2)}) collective-permute-start(bf16[6,128,768]{2,1,0:T(8,128)(2,1)} %get-tuple-element.81), channel_id=1, source_target_pairs={{0,1},{1,0},{2,3},{3,2},{4,5},{5,4},{6,7},{7,6}} | collective-permute-start | bytes 3538952 | tf_op jit(solution)/shard_map/ppermute | solution.py:621
  446.8 3.2 collective-permute-start.5
  446.8 4.8 %collective-permute-start.6 = (bf16[6,128,768]{2,1,0:T(8,128)(2,1)}, bf16[6,128,768]{2,1,0:T(8,128)(2,1)}, u32[]{:S(2)}, u32[]{:S(2)}) collective-permute-start(bf16[6,128,768]{2,1,0:T(8,128)(2,1)} %get-tuple-element.79), channel_id=1, source_target_pairs={{0,1},{1,0},{2,3},{3,2},{4,5},{5,4},{6,7},{7,6}} | collective-permute-start | bytes 3538952 | tf_op jit(solution)/shard_map/ppermute | solution.py:621

commit v4 on v3

--- a/solution.py
+++ b/solution.py
@@ -217,17 +217,13 @@
 
     lax.fori_loop(0, B // 128, zero_c, 0)
 
-    def gelu_dot(zf, rows):
+    def gelu_dot(zf, rows, i):
         u = (zf * (0.5 + 0.5 * lax.erf(zf * SQRT_HALF))).astype(BF16)
-        acc_d[...] += dot(u, bbuf[rows, :], ((0,), (0,)))
+        acc_d[...] = jnp.where(i == 0, 0.0, acc_d[...]) + dot(u, bbuf[rows, :], ((0,), (0,)))
 
     def pass_one(s, i):
         slot = lax.rem(s, 2)
         rows = rows_of(i * R, R)
-
-        @pl.when(i == 0)
-        def _():
-            acc_d[...] = jnp.zeros_like(acc_d)
 
         @pl.when(s < NB)
         def _():
@@ -243,34 +239,30 @@
 
             z = dot(abuf[rows, :], wa[slot], ((1,), (0,))).astype(BF16)
             zb[rows, :] = z
-            gelu_dot(z.astype(F32), rows)
+            gelu_dot(z.astype(F32), rows, i)
 
         @pl.when(s >= NB)
         def _():
             for c in z_copies(s, i):
                 c.wait()
-            gelu_dot(zb[rows, :].astype(F32), rows)
-
-    def slope_dot(s, rows):
+            gelu_dot(zb[rows, :].astype(F32), rows, i)
+
+    def slope_dot(s, rows, i):
         slot = lax.rem(s, 2)
         e = dot(bbuf[rows, :], wb[slot], ((1,), (1,))).astype(BF16)
         zf = zb[rows, :].astype(F32)
         slope = 0.5 + 0.5 * lax.erf(zf * SQRT_HALF) + zf * jnp.exp2(zf * zf * EXP_SCALE) * PDF_SCALE
         dd = (e.astype(F32) * slope).astype(BF16)
-        acc_u[...] += dot(abuf[rows, :], dd, ((0,), (0,)))
+        acc_u[...] = jnp.where(i == 0, 0.0, acc_u[...]) + dot(abuf[rows, :], dd, ((0,), (0,)))
         return dd
 
     def pass_two(s, i):
         slot = lax.rem(s, 2)
         rows = rows_of(i * R, R)
 
-        @pl.when(i == 0)
-        def _():
-            acc_u[...] = jnp.zeros_like(acc_u)
-
         @pl.when(s < NB)
         def _():
-            dd = slope_dot(s, rows)
+            dd = slope_dot(s, rows, i)
             cbuf[rows, :] += dot(dd, wa[slot], ((1,), (1,)))
 
         @pl.when(s >= NB)
@@ -279,17 +271,17 @@
             def _():
                 row_copy(x_hbm, abuf, asem, i).wait()
 
-            slope_dot(s, rows)
+            slope_dot(s, rows, i)
 
         @pl.when(jnp.logical_and(s + 1 >= NB, s + 1 < STEPS))
         def _():
             for c in z_copies(s + 1, i):
                 c.start()
 
-    plans = (((item_d, 2, 1), (item_d, 4, 2)),
-             ((item_u, 1, 1), (item_u, 3, 2), (item_u, 5, 3), (item_d, 0, 0)),
-             ((item_d, 1, 0), (item_d, 3, 1), (item_d, 5, 2)),
-             ((item_u, 2, 1), (item_u, 4, 2), (item_u, 0, 0)))
+    plans = (((item_u, 1, 1), (item_d, 4, 2)),
+             ((item_d, 2, 1), (item_u, 3, 2), (item_d, 0, 0)),
+             ((item_d, 1, 0), (item_d, 3, 1), (item_u, 5, 3)),
+             ((item_u, 2, 1), (item_u, 4, 2), (item_d, 5, 2), (item_u, 0, 0)))
 
     def quarter(t, carry):
         s = lax.div(t, 4)
@@ -576,45 +568,53 @@
     )(stats, *grads, *states, *prev)
 
 
-def place_kernel(w, j0, nj, got_u, got_d, _u, _d, out_u, out_d, buf_u, buf_d, sem_in, sem_out):
+def place_kernel(parts, *refs):
+    n_in = 2 * len(parts)
+    got, (out_u, out_d), refs = refs[:n_in], refs[n_in + 2:n_in + 4], refs[n_in + 4:]
     q = 1 - lax.axis_index('data')
     rows = pl.ds(pl.multiple_of(q * (D // 2), 8), D // 2)
-    loads, stores = [], []
-    for p in range(2):
-        loads.append(pltpu.make_async_copy(got_u.at[p], buf_u.at[p], sem_in.at[p]))
-        stores.append(pltpu.make_async_copy(buf_u.at[p], out_u.at[w, rows, pl.ds((p * NB + j0) * HB, nj * HB)], sem_out.at[p]))
-    for p in range(2):
-        part = pl.ds(p * nj, nj)
-        loads.append(pltpu.make_async_copy(got_d.at[part], buf_d.at[part], sem_in.at[2 + p]))
-        for i in range(nj):
-            t = p * nj + i
-            to = pl.ds(pl.multiple_of(q * (FF // 2) + (t + 2 * j0) * 128, 8), 128)
-            stores.append(pltpu.make_async_copy(buf_d.at[t], out_d.at[w, to, :], sem_out.at[2 + t]))
-    for c in loads:
-        c.start()
-    for k, c in enumerate(loads):
-        c.wait()
-        for st in stores[k:k + 1] if k < 2 else stores[2 + (k - 2) * nj:2 + (k - 1) * nj]:
+    moves = []
+    for k, (w, j0, nj) in enumerate(parts):
+        buf_u, buf_d, sem_in, sem_out = refs[4 * k:4 * k + 4]
+        for p in range(2):
+            moves.append((pltpu.make_async_copy(got[2 * k].at[p], buf_u.at[p], sem_in.at[p]), [
+                pltpu.make_async_copy(buf_u.at[p], out_u.at[w, rows, pl.ds((p * NB + j0) * HB, nj * HB)], sem_out.at[p])]))
+        for p in range(2):
+            part = pl.ds(p * nj, nj)
+            stores = []
+            for t in range(p * nj, (p + 1) * nj):
+                to = pl.ds(pl.multiple_of(q * (FF // 2) + (t + 2 * j0) * 128, 8), 128)
+                stores.append(pltpu.make_async_copy(buf_d.at[t], out_d.at[w, to, :], sem_out.at[2 + t]))
+            moves.append((pltpu.make_async_copy(got[2 * k + 1].at[part], buf_d.at[part], sem_in.at[2 + p]), stores))
+    for load, stores in moves:
+        load.start()
+    for load, stores in moves:
+        load.wait()
+        for st in stores:
             st.start()
-    for st in stores:
-        st.wait()
-
-
-def place(w, j0, nj, got, weights):
+    for load, stores in moves:
+        for st in stores:
+            st.wait()
+
+
+def place(parts, got, weights):
     any_spec = pl.BlockSpec(memory_space=pl.ANY)
-    n = 2 * nj
-    cells = D * nj * HB * 2
+    flat = [v for pair in got for v in pair]
+    scratch = []
+    for w, j0, nj in parts:
+        scratch += [pltpu.VMEM((2, D // 2, nj * HB), BF16), pltpu.VMEM((2 * nj, 128, D), BF16),
+                    pltpu.SemaphoreType.DMA((4,)), pltpu.SemaphoreType.DMA((2 + 2 * nj,))]
+    cells = sum(D * nj * HB * 2 for w, j0, nj in parts)
     return pl.pallas_call(
-        lambda *refs: place_kernel(w, j0, nj, *refs),
+        lambda *refs: place_kernel(parts, *refs),
         out_shape=(jax.ShapeDtypeStruct((2, D, FF), BF16), jax.ShapeDtypeStruct((2, FF, D), BF16)),
-        in_specs=[any_spec] * 4,
+        in_specs=[any_spec] * (len(flat) + 2),
         out_specs=(any_spec, any_spec),
-        scratch_shapes=[pltpu.VMEM((2, D // 2, nj * HB), BF16), pltpu.VMEM((n, 128, D), BF16),
-                        pltpu.SemaphoreType.DMA((4,)), pltpu.SemaphoreType.DMA((2 + n,))],
-        input_output_aliases={2 + k: k for k in range(2)},
+        scratch_shapes=scratch,
+        input_output_aliases={len(flat) + k: k for k in range(2)},
         compiler_params=pltpu.CompilerParams(vmem_limit_bytes=67043328),
         cost_estimate=pl.CostEstimate(flops=cells * 100, bytes_accessed=cells * 4, transcendentals=0),
-    )(*got, *weights)
+    )(*flat, *weights)
 
 
 def swap(halves):
@@ -642,11 +642,10 @@
         got_a = swap([wu, wd])
         *new, wu, wd = adam(stats, [g_up, g_down], states, new, 0, 0, cut)
         got_b = swap([wu, wd])
-        new[6:] = place(1, 0, NB, got_a, new[6:])
         *new, wu, wd = adam(stats, tails, states, new, 0, cut, TAIL, tail=True)
         got_c = swap([wu, wd])
-        new[6:] = place(0, 0, cut, got_b, new[6:])
-        new[6:] = place(0, cut, TAIL, got_c, new[6:])
+        new[6:] = place([(1, 0, NB), (0, 0, cut)], [got_a, got_b], new[6:])
+        new[6:] = place([(0, cut, TAIL)], [got_c], new[6:])
         m_up, o_up, v_up, m_down, o_down, v_down, new_up, new_down = new
         return (new_up, new_down, m_up, m_down, o_up, o_down, v_up, v_down, norm.reshape(()))
 

time: 455 us -> 424 us (0.932)
  waiting for transfers between devices: 28.6 us -> 1.02 us
    ppermute x2, waiting for transfers between devices: 26.8 us -> 0.07 us  [device_step(): tails.append(lax.ppermute(g_tail, axes, perm))]
  transfers between devices with their start and end apart: 9 -> 9, of which waited for: 3 -> 2; matrix products, arithmetic and copies ran while one was open for 0% -> 0% of each run, Pallas kernels for 8% -> 15%
where the time goes in v4:
time: 424 us
  Pallas kernels  417 us (98%)
    pallas_call x1, Pallas kernels, backward_reduce(): pl.pallas_call(mega_kernel, out_shape=(jax.ShapeDtypeStruct((2, NB, D //...  307 us
    pallas_call x3, Pallas kernels, adam(): pl.pallas_call(lambda *refs: adam_kernel(w, j0, nj, tail, len(prev), *ref...  55.7 us
    pallas_call x1, Pallas kernels, forward(): pl.pallas_call(forward_body, grid=(B // rows,), out_shape=(jax.ShapeDtype...  45.9 us
    pallas_call x2, Pallas kernels, place(): pl.pallas_call(lambda *refs: place_kernel(parts, *refs), out_shape=(jax.S...  8.56 us
  transfers between devices with their start and end apart: 9, of which 2 were waited for; matrix products, arithmetic and copies ran while one was open for 0% of the time, Pallas kernels for 15%

profile of v4, /device:TPU:0, one launch (start us, length us, event | category | flops | bytes accessed | tf_op | source)
XLA Modules:
  0.0 423.6 jit_solution(10419136918550738987)
XLA Ops:
  1.3 45.9 %forward.1 = (bf16[4096,3072]{1,0:T(8,128)(2,1)}, bf16[4096,768]{1,0:T(8,128)(2,1)}) custom-call(bf16[4096,768]{1,0:T(8,128)(2,1)} %x_hbm.1, bf16[2,768,3072]{2,1,0:T(8,128)(2,1)} %wu_hbm.1, bf16[2,3072,768]{2,1,0:T(8,128)(2,1)} %wd_hbm.1), custom_call_target="tpu_custom_call" | custom-call | tf_op jit(solution)/shard_map/forward/pallas_call | solution.py:406
  47.2 306.7 %backward_reduce.1 = (f32[2,6,384,512]{3,2,1,0:T(8,128)}, f32[2,1536,768]{2,1,0:T(8,128)}, f32[3,2,192,256]{3,2,1,0:T(8,128)}, f32[2,8,128]{2,1,0:T(8,128)}) custom-call(f32[1]{0:T(128)} %bitcast.2.clip_ref, bf16[4096,768]{1,0:T(8,128)(2,1)} %get-tuple-element.50.h_hbm, bf16[4096,768]{1,0:T(8,128)(2,1)} %dy_hbm.1, bf16[4096,768]{1,0:T(8,128)(2,1)} %x_hbm.1, ...), custom_call_target="tpu_custom_call" | custom-call | tf_op jit(solution)/shard_map/backward_reduce/pallas_call | solution.py:377
  353.9 0.7 collective-permute-start
  354.6 1.5 collective-permute-start.1
  356.1 26.4 %shard_map.178 = (f32[2,384,3072]{2,1,0:T(8,128)}, f32[2,384,3072]{2,1,0:T(8,128)}, f32[2,384,3072]{2,1,0:T(8,128)}, f32[2,1536,768]{2,1,0:T(8,128)}, f32[2,1536...) custom-call(f32[2,8,128]{2,1,0:T(8,128)} %get-tuple-element.52.refs_, ...), custom_call_target="tpu_custom_call" | custom-call | flops 943718400 | bytes 70778880 | tf_op jit(solution)/shard_map/pallas_call | solution.py:555
  382.5 0.0 collective-permute-start.5
  382.5 0.1 collective-permute-done.refs_2_
  382.6 0.9 collective-permute-start.2
  383.5 0.0 collective-permute-start.6
  383.5 14.1 %shard_map.179 = (f32[2,384,3072]{2,1,0:T(8,128)}, f32[2,384,3072]{2,1,0:T(8,128)}, f32[2,384,3072]{2,1,0:T(8,128)}, f32[2,1536,768]{2,1,0:T(8,128)}, f32[2,1536...) custom-call(f32[2,8,128]{2,1,0:T(8,128)} %get-tuple-element.52.refs_, ...), custom_call_target="tpu_custom_call", output_to_operand_aliasing={{0}: (9, {}), {1}: (10, {}), {2}: (11, {}), {3}: (12, {}), ... | custom-call | flops 471859200 | bytes 35389440 | tf_op jit(solution)/shard_map/pallas_call | solution.py:555
  397.6 0.5 collective-permute-start.7
  398.1 0.0 collective-permute-done.1.refs_3_
  398.1 0.0 collective-permute-start.8
  398.2 0.9 collective-permute-done.2.refs_4_
  399.1 15.2 %shard_map.180 = (f32[2,384,3072]{2,1,0:T(8,128)}, f32[2,384,3072]{2,1,0:T(8,128)}, f32[2,384,3072]{2,1,0:T(8,128)}, f32[2,1536,768]{2,1,0:T(8,128)}, f32[2,1536...) custom-call(f32[2,8,128]{2,1,0:T(8,128)} %get-tuple-element.52.refs_, ...), custom_call_target="tpu_custom_call", output_to_operand_aliasing={{0}: (11, {}), {1}: (12, {}), {2}: (13, {}), {3}: (14, {}),... | custom-call | flops 471859200 | bytes 35389440 | tf_op jit(solution)/shard_map/pallas_call | solution.py:555
  414.3 0.0 collective-permute-start.3
  414.3 0.0 collective-permute-done.7.refs_2_
  414.3 0.5 collective-permute-start.4
  414.8 0.0 collective-permute-done.8.refs_3_
  414.8 0.0 collective-permute-done.5.refs_0_
  414.8 0.0 collective-permute-done.6.refs_1_
  414.8 6.0 %shard_map.181 = (bf16[2,768,3072]{2,1,0:T(8,128)(2,1)}, bf16[2,3072,768]{2,1,0:T(8,128)(2,1)}) custom-call(bf16[2,384,1536]{2,1,0:T(8,128)(2,1)} %collective-permute-done.5.refs_0_, bf16[12,128,768]{2,1,0:T(8,128)(2,1)} %collective-permute-done.6.refs_1_, ...), custom_call_target="tpu_custom_call", output_to_operand_aliasing={{0}: (4, {}), {1}: (5, {})} | custom-call | flops 353894400 | bytes 14155776 | tf_op jit(solution)/shard_map/pallas_call | solution.py:608
  420.8 0.0 collective-permute-done.3.refs_0_
  420.8 0.0 collective-permute-done.4.refs_1_
  420.9 2.6 shard_map.182
Async XLA Ops:
  353.9 28.7 %collective-permute-start = (f32[3,2,192,256]{3,2,1,0:T(8,128)}, f32[3,2,192,256]{3,2,1,0:T(8,128)}, u32[]{:S(2)}, u32[]{:S(2)}) collective-permute-start(f32[3,2,192,256]{3,2,1,0:T(8,128)} %get-tuple-element.53.refs_1_), channel_id=1, source_target_pairs={{0,4},{1,3},{2,6},{3,1},{4,0},{5,7},{6,2},{7,5}} | collective-permute-start | bytes 3538952 | tf_op jit(solution)/shard_map/ppermute | solution.py:637
  354.6 43.5 %collective-permute-start.1 = (f32[3,2,192,256]{3,2,1,0:T(8,128)}, f32[3,2,192,256]{3,2,1,0:T(8,128)}, u32[]{:S(2)}, u32[]{:S(2)}) collective-permute-start(f32[3,2,192,256]{3,2,1,0:T(8,128)} %get-tuple-element.53.refs_1_), channel_id=1, source_target_pairs={{0,2},{1,5},{2,0},{3,7},{4,6},{5,1},{6,4},{7,3}} | collective-permute-start | bytes 3538952 | tf_op jit(solution)/shard_map/ppermute | solution.py:637
  382.5 32.3 %collective-permute-start.5 = (bf16[2,384,1536]{2,1,0:T(8,128)(2,1)}, bf16[2,384,1536]{2,1,0:T(8,128)(2,1)}, u32[]{:S(2)}, u32[]{:S(2)}) collective-permute-start(bf16[2,384,1536]{2,1,0:T(8,128)(2,1)} %get-tuple-element.74), channel_id=1, source_target_pairs={{0,1},{1,0},{2,3},{3,2},{4,5},{5,4},{6,7},{7,6}} | collective-permute-start | bytes 7077896 | tf_op jit(solution)/shard_map/ppermute | solution.py:621
  382.6 16.5 %collective-permute-start.2 = (f32[3,2,192,256]{3,2,1,0:T(8,128)}, f32[3,2,192,256]{3,2,1,0:T(8,128)}, u32[]{:S(2)}, u32[]{:S(2)}) collective-permute-start(f32[3,2,192,256]{3,2,1,0:T(8,128)} %collective-permute-done.refs_2_), channel_id=1, source_target_pairs={{0,2},{1,5},{2,0},{3,7},{4,6},{5,1},{6,4},{7,3}} | collective-permute-start | bytes 3538952 | tf_op jit(solution)/shard_map/ppermute | solution.py:638
  383.5 31.4 %collective-permute-start.6 = (bf16[12,128,768]{2,1,0:T(8,128)(2,1)}, bf16[12,128,768]{2,1,0:T(8,128)(2,1)}, u32[]{:S(2)}, u32[]{:S(2)}) collective-permute-start(bf16[12,128,768]{2,1,0:T(8,128)(2,1)} %get-tuple-element.75), channel_id=1, source_target_pairs={{0,1},{1,0},{2,3},{3,2},{4,5},{5,4},{6,7},{7,6}} | collective-permute-start | bytes 7077896 | tf_op jit(solution)/shard_map/ppermute | solution.py:621
  397.6 16.7 %collective-permute-start.7 = (bf16[2,384,768]{2,1,0:T(8,128)(2,1)}, bf16[2,384,768]{2,1,0:T(8,128)(2,1)}, u32[]{:S(2)}, u32[]{:S(2)}) collective-permute-start(bf16[2,384,768]{2,1,0:T(8,128)(2,1)} %get-tuple-element.76), channel_id=1, source_target_pairs={{0,1},{1,0},{2,3},{3,2},{4,5},{5,4},{6,7},{7,6}} | collective-permute-start | bytes 3538952 | tf_op jit(solution)/shard_map/ppermute | solution.py:621
  398.1 16.7 %collective-permute-start.8 = (bf16[6,128,768]{2,1,0:T(8,128)(2,1)}, bf16[6,128,768]{2,1,0:T(8,128)(2,1)}, u32[]{:S(2)}, u32[]{:S(2)}) collective-permute-start(bf16[6,128,768]{2,1,0:T(8,128)(2,1)} %get-tuple-element.77), channel_id=1, source_target_pairs={{0,1},{1,0},{2,3},{3,2},{4,5},{5,4},{6,7},{7,6}} | collective-permute-start | bytes 3538952 | tf_op jit(solution)/shard_map/ppermute | solution.py:621
  414.3 6.6 %collective-permute-start.3 = (bf16[2,384,768]{2,1,0:T(8,128)(2,1)}, bf16[2,384,768]{2,1,0:T(8,128)(2,1)}, u32[]{:S(2)}, u32[]{:S(2)}) collective-permute-start(bf16[2,384,768]{2,1,0:T(8,128)(2,1)} %get-tuple-element.72), channel_id=1, source_target_pairs={{0,1},{1,0},{2,3},{3,2},{4,5},{5,4},{6,7},{7,6}} | collective-permute-start | bytes 3538952 | tf_op jit(solution)/shard_map/ppermute | solution.py:621
  414.3 6.5 %collective-permute-start.4 = (bf16[6,128,768]{2,1,0:T(8,128)(2,1)}, bf16[6,128,768]{2,1,0:T(8,128)(2,1)}, u32[]{:S(2)}, u32[]{:S(2)}) collective-permute-start(bf16[6,128,768]{2,1,0:T(8,128)(2,1)} %get-tuple-element.73), channel_id=1, source_target_pairs={{0,1},{1,0},{2,3},{3,2},{4,5},{5,4},{6,7},{7,6}} | collective-permute-start | bytes 3538952 | tf_op jit(solution)/shard_map/ppermute | solution.py:621

commit v5 on v4

--- a/solution.py
+++ b/solution.py
@@ -19,6 +19,8 @@
 BF16 = jnp.bfloat16
 
 B, D, FF = 4096, 768, 3072
+HD, HF = D // 2, FF // 2
+NN, NT, TN = ((1,), (0,)), ((1,), (1,)), ((0,), (0,))
 NB = 6
 HB = FF // NB // 2
 BF = 2 * HB
@@ -69,7 +71,7 @@
     b = (1 - d) * y + d * x
 
     item_d = Item(HB, D, (acc_d, r0_d, r1_d, r2_d, h_d), (send_d, recv_d, loc_d))
-    item_u = Item(D // 2, BF, (acc_u, r0_u, r1_u, r2_u, h_u), (send_u, recv_u, loc_u))
+    item_u = Item(HD, BF, (acc_u, r0_u, r1_u, r2_u, h_u), (send_u, recv_u, loc_u))
 
     def rows_of(start, size):
         return pl.ds(pl.multiple_of(start, 8), size)
@@ -84,7 +86,7 @@
         ph = 1 - lax.div(s, NB)
         up, down = [], []
         for p in range(2):
-            cols = pl.ds(pl.multiple_of(p * (FF // 2) + j * HB, 128), HB)
+            cols = pl.ds(pl.multiple_of(p * HF + j * HB, 128), HB)
             up.append(pltpu.make_async_copy(wu_hbm.at[1, :, cols], wa.at[slot, :, p * HB:(p + 1) * HB], wsem.at[slot, p]))
             down.append(pltpu.make_async_copy(wd_hbm.at[ph, cols, :], wb.at[slot, p * HB:(p + 1) * HB, :], wsem.at[slot, 2 + p]))
         return up, down
@@ -93,7 +95,7 @@
         j = lax.rem(s, NB)
         out = []
         for p in range(2):
-            cols = pl.ds(pl.multiple_of(p * (FF // 2) + j * HB, 128), HB)
+            cols = pl.ds(pl.multiple_of(p * HF + j * HB, 128), HB)
             rows = rows_of(i * R, R)
             out.append(pltpu.make_async_copy(z_hbm.at[rows, cols], zb.at[rows, p * HB:(p + 1) * HB], zsem.at[i, p]))
         return out
@@ -203,12 +205,10 @@
         c.start()
 
     barrier = pltpu.get_barrier_semaphore()
-    for fy in range(2):
-        for fx in range(2):
-            for fd in range(2):
-                if fy + fx + fd:
-                    dev = (2 * (y + fy - 2 * fy * y) + x + fx - 2 * fx * x, d + fd - 2 * fd * d)
-                    pl.semaphore_signal(barrier, inc=1, device_id=dev, device_id_type=MESH)
+    peers = [(2 * (y + fy - 2 * fy * y) + x + fx - 2 * fx * x, d + fd - 2 * fd * d)
+             for fy in range(2) for fx in range(2) for fd in range(2)]
+    for dev in peers[1:]:
+        pl.semaphore_signal(barrier, inc=1, device_id=dev, device_id_type=MESH)
     pl.semaphore_wait(barrier, 7)
 
     def zero_c(i, carry):
@@ -219,7 +219,7 @@
 
     def gelu_dot(zf, rows, i):
         u = (zf * (0.5 + 0.5 * lax.erf(zf * SQRT_HALF))).astype(BF16)
-        acc_d[...] = jnp.where(i == 0, 0.0, acc_d[...]) + dot(u, bbuf[rows, :], ((0,), (0,)))
+        acc_d[...] = jnp.where(i == 0, 0.0, acc_d[...]) + dot(u, bbuf[rows, :], TN)
 
     def pass_one(s, i):
         slot = lax.rem(s, 2)
@@ -237,7 +237,7 @@
                     row_copy(h_hbm, abuf, asem, i + 1).start()
                     row_copy(dy_hbm, bbuf, bsem, i + 1).start()
 
-            z = dot(abuf[rows, :], wa[slot], ((1,), (0,))).astype(BF16)
+            z = dot(abuf[rows, :], wa[slot], NN).astype(BF16)
             zb[rows, :] = z
             gelu_dot(z.astype(F32), rows, i)
 
@@ -249,11 +249,11 @@
 
     def slope_dot(s, rows, i):
         slot = lax.rem(s, 2)
-        e = dot(bbuf[rows, :], wb[slot], ((1,), (1,))).astype(BF16)
+        e = dot(bbuf[rows, :], wb[slot], NT).astype(BF16)
         zf = zb[rows, :].astype(F32)
         slope = 0.5 + 0.5 * lax.erf(zf * SQRT_HALF) + zf * jnp.exp2(zf * zf * EXP_SCALE) * PDF_SCALE
         dd = (e.astype(F32) * slope).astype(BF16)
-        acc_u[...] = jnp.where(i == 0, 0.0, acc_u[...]) + dot(abuf[rows, :], dd, ((0,), (0,)))
+        acc_u[...] = jnp.where(i == 0, 0.0, acc_u[...]) + dot(abuf[rows, :], dd, TN)
         return dd
 
     def pass_two(s, i):
@@ -263,7 +263,7 @@
         @pl.when(s < NB)
         def _():
             dd = slope_dot(s, rows, i)
-            cbuf[rows, :] += dot(dd, wa[slot], ((1,), (1,)))
+            cbuf[rows, :] += dot(dd, wa[slot], NT)
 
         @pl.when(s >= NB)
         def _():
@@ -338,8 +338,6 @@
 
     lax.fori_loop(0, 4 * (STEPS + 1) + 2, quarter, 0)
 
-    peers = [(2 * (y + fy - 2 * fy * y) + x + fx - 2 * fx * x, d + fd - 2 * fd * d)
-             for fy in range(2) for fx in range(2) for fd in range(2)]
     sq_in[0] = ssq[0]
     for t in range(FULL, STEPS):
         for it in (item_d, item_u):
@@ -376,15 +374,15 @@
     dma = pltpu.SemaphoreType.DMA
     return pl.pallas_call(
         mega_kernel,
-        out_shape=(jax.ShapeDtypeStruct((2, NB, D // 2, BF), F32),
-                   jax.ShapeDtypeStruct((2, FF // 2, D), F32),
+        out_shape=(jax.ShapeDtypeStruct((2, NB, HD, BF), F32),
+                   jax.ShapeDtypeStruct((2, HF, D), F32),
                    jax.ShapeDtypeStruct((TAIL, 2, 192, 256), F32),
                    jax.ShapeDtypeStruct((2, 8, 128), F32)),
         in_specs=[pl.BlockSpec(memory_space=pltpu.SMEM)] + [any_spec] * 6,
         out_specs=(any_spec, any_spec, any_spec, pl.BlockSpec(memory_space=pltpu.VMEM)),
         scratch_shapes=[vmem((B, D), BF16), vmem((B, D), BF16), vmem((B, D), F32),
                         vmem((2, D, BF), BF16), vmem((2, BF, D), BF16), vmem((B, BF), BF16)]
-        + item(HB, D, (BF, D)) + item(D // 2, BF, (D, BF))
+        + item(HB, D, (BF, D)) + item(HD, BF, (D, BF))
         + [vmem((1, 8, 128), F32), vmem((8, 8, 128), F32)]
         + [dma((NCH,)), dma((NCH,)), dma((2, 4)), dma((NCH, 2)), dma((TAIL, 2, 3)), dma((8,)), dma((8,))]
         + [dma((5, SLOTS)), dma((5, SLOTS)), dma((SLOTS,))] * 2,
@@ -394,10 +392,10 @@
 
 
 def forward_body(x, wu, wd, z_ref, h_ref):
-    z = dot(x[...], wu[0], ((1,), (0,))).astype(BF16)
+    z = dot(x[...], wu[0], NN).astype(BF16)
     z_ref[...] = z
     u = gelu_value(z.astype(F32)).astype(BF16)
-    h_ref[...] = dot(u, wd[0], ((1,), (0,))).astype(BF16)
+    h_ref[...] = dot(u, wd[0], NN).astype(BF16)
 
 
 def forward(x, w_up, w_down):
@@ -425,7 +423,7 @@
 
 def adam_kernel(w, j0, nj, tail, n_alias, stats, *refs):
     n = 2 * nj
-    ru = D // 2 // n
+    ru = HD // n
     n_grads = 4 if tail else 2
     grads, refs = refs[:n_grads], refs[n_grads:]
     states, refs = refs[:6], refs[6 + n_alias:]
@@ -463,8 +461,8 @@
                 cs.append(pltpu.make_async_copy(out_u.at[k, q, p], up_at(outs[q], p, i * ru, ru), osem.at[k, 2 * q + p]))
             cs.append(pltpu.make_async_copy(out_d.at[k, q], outs[3 + q].at[w, row, :], osem.at[k, 6 + q]))
         for p in range(2):
-            cs.append(pltpu.make_async_copy(w_u.at[k, p], up_at(outs[6], p, d * (D // 2) + i * ru, ru), osem.at[k, 9 + p]))
-        my_down = pl.ds(pl.multiple_of(d * (FF // 2) + (i + 2 * j0) * 128, 8), 128)
+            cs.append(pltpu.make_async_copy(w_u.at[k, p], up_at(outs[6], p, d * HD + i * ru, ru), osem.at[k, 9 + p]))
+        my_down = pl.ds(pl.multiple_of(d * HF + (i + 2 * j0) * 128, 8), 128)
         cs.append(pltpu.make_async_copy(w_d.at[k], outs[7].at[w, my_down, :], osem.at[k, 11]))
         cs.append(pltpu.make_async_copy(w_u.at[k], outs[8].at[:, pl.ds(pl.multiple_of(i * ru, 8), ru), :], osem.at[k, 12]))
         cs.append(pltpu.make_async_copy(w_d.at[k], outs[9].at[i], osem.at[k, 13]))
@@ -544,10 +542,10 @@
 def adam(stats, grads, states, prev, w, j0, nj, tail=False):
     any_spec = pl.BlockSpec(memory_space=pl.ANY)
     n = 2 * nj
-    ru = D // 2 // n
+    ru = HD // n
     full = [jax.ShapeDtypeStruct(v.shape, F32) for v in states]
     whole = [jax.ShapeDtypeStruct((2, D, FF), BF16), jax.ShapeDtypeStruct((2, FF, D), BF16)]
-    halves = [jax.ShapeDtypeStruct((2, D // 2, nj * HB), BF16), jax.ShapeDtypeStruct((n, 128, D), BF16)]
+    halves = [jax.ShapeDtypeStruct((2, HD, nj * HB), BF16), jax.ShapeDtypeStruct((n, 128, D), BF16)]
     norm = [] if prev else [jax.ShapeDtypeStruct((1,), F32)]
     first = 1 + len(grads) + 6
     cells = D * nj * HB * 2
@@ -572,7 +570,7 @@
     n_in = 2 * len(parts)
     got, (out_u, out_d), refs = refs[:n_in], refs[n_in + 2:n_in + 4], refs[n_in + 4:]
     q = 1 - lax.axis_index('data')
-    rows = pl.ds(pl.multiple_of(q * (D // 2), 8), D // 2)
+    rows = pl.ds(pl.multiple_of(q * HD, 8), HD)
     moves = []
     for k, (w, j0, nj) in enumerate(parts):
         buf_u, buf_d, sem_in, sem_out = refs[4 * k:4 * k + 4]
@@ -583,7 +581,7 @@
             part = pl.ds(p * nj, nj)
             stores = []
             for t in range(p * nj, (p + 1) * nj):
-                to = pl.ds(pl.multiple_of(q * (FF // 2) + (t + 2 * j0) * 128, 8), 128)
+                to = pl.ds(pl.multiple_of(q * HF + (t + 2 * j0) * 128, 8), 128)
                 stores.append(pltpu.make_async_copy(buf_d.at[t], out_d.at[w, to, :], sem_out.at[2 + t]))
             moves.append((pltpu.make_async_copy(got[2 * k + 1].at[part], buf_d.at[part], sem_in.at[2 + p]), stores))
     for load, stores in moves:
@@ -602,7 +600,7 @@
     flat = [v for pair in got for v in pair]
     scratch = []
     for w, j0, nj in parts:
-        scratch += [pltpu.VMEM((2, D // 2, nj * HB), BF16), pltpu.VMEM((2 * nj, 128, D), BF16),
+        scratch += [pltpu.VMEM((2, HD, nj * HB), BF16), pltpu.VMEM((2 * nj, 128, D), BF16),
                     pltpu.SemaphoreType.DMA((4,)), pltpu.SemaphoreType.DMA((2 + 2 * nj,))]
     cells = sum(D * nj * HB * 2 for w, j0, nj in parts)
     return pl.pallas_call(

time: 424 us -> 424 us (level)
  no operation moved by 1% of the time
where the time goes in v5:
time: 424 us
  Pallas kernels  417 us (98%)
    pallas_call x1, Pallas kernels, backward_reduce(): pl.pallas_call(mega_kernel, out_shape=(jax.ShapeDtypeStruct((2, NB, HD, B...  307 us
    pallas_call x3, Pallas kernels, adam(): pl.pallas_call(lambda *refs: adam_kernel(w, j0, nj, tail, len(prev), *ref...  55.7 us
    pallas_call x1, Pallas kernels, forward(): pl.pallas_call(forward_body, grid=(B // rows,), out_shape=(jax.ShapeDtype...  45.9 us
    pallas_call x2, Pallas kernels, place(): pl.pallas_call(lambda *refs: place_kernel(parts, *refs), out_shape=(jax.S...  8.56 us
  transfers between devices with their start and end apart: 9, of which 2 were waited for; matrix products, arithmetic and copies ran while one was open for 0% of the time, Pallas kernels for 15%

profile of v5, /device:TPU:0, one launch (start us, length us, event | category | flops | bytes accessed | tf_op | source)
XLA Modules:
  0.0 423.6 jit_solution(9296696516482940775)
XLA Ops:
  1.3 45.9 %forward.1 = (bf16[4096,3072]{1,0:T(8,128)(2,1)}, bf16[4096,768]{1,0:T(8,128)(2,1)}) custom-call(bf16[4096,768]{1,0:T(8,128)(2,1)} %x_hbm.1, bf16[2,768,3072]{2,1,0:T(8,128)(2,1)} %wu_hbm.1, bf16[2,3072,768]{2,1,0:T(8,128)(2,1)} %wd_hbm.1), custom_call_target="tpu_custom_call" | custom-call | tf_op jit(solution)/shard_map/forward/pallas_call | solution.py:404
  47.2 306.7 %backward_reduce.1 = (f32[2,6,384,512]{3,2,1,0:T(8,128)}, f32[2,1536,768]{2,1,0:T(8,128)}, f32[3,2,192,256]{3,2,1,0:T(8,128)}, f32[2,8,128]{2,1,0:T(8,128)}) custom-call(f32[1]{0:T(128)} %bitcast.2.clip_ref, bf16[4096,768]{1,0:T(8,128)(2,1)} %get-tuple-element.50.h_hbm, bf16[4096,768]{1,0:T(8,128)(2,1)} %dy_hbm.1, bf16[4096,768]{1,0:T(8,128)(2,1)} %x_hbm.1, ...), custom_call_target="tpu_custom_call" | custom-call | tf_op jit(solution)/shard_map/backward_reduce/pallas_call | solution.py:375
  353.9 0.7 collective-permute-start
  354.6 1.5 collective-permute-start.1
  356.1 26.4 %shard_map.178 = (f32[2,384,3072]{2,1,0:T(8,128)}, f32[2,384,3072]{2,1,0:T(8,128)}, f32[2,384,3072]{2,1,0:T(8,128)}, f32[2,1536,768]{2,1,0:T(8,128)}, f32[2,1536...) custom-call(f32[2,8,128]{2,1,0:T(8,128)} %get-tuple-element.52.refs_, ...), custom_call_target="tpu_custom_call" | custom-call | flops 943718400 | bytes 70778880 | tf_op jit(solution)/shard_map/pallas_call | solution.py:553
  382.5 0.0 collective-permute-start.5
  382.5 0.1 collective-permute-done.refs_2_
  382.6 0.9 collective-permute-start.2
  383.5 0.0 collective-permute-start.6
  383.5 14.1 %shard_map.179 = (f32[2,384,3072]{2,1,0:T(8,128)}, f32[2,384,3072]{2,1,0:T(8,128)}, f32[2,384,3072]{2,1,0:T(8,128)}, f32[2,1536,768]{2,1,0:T(8,128)}, f32[2,1536...) custom-call(f32[2,8,128]{2,1,0:T(8,128)} %get-tuple-element.52.refs_, ...), custom_call_target="tpu_custom_call", output_to_operand_aliasing={{0}: (9, {}), {1}: (10, {}), {2}: (11, {}), {3}: (12, {}), ... | custom-call | flops 471859200 | bytes 35389440 | tf_op jit(solution)/shard_map/pallas_call | solution.py:553
  397.6 0.5 collective-permute-start.7
  398.1 0.0 collective-permute-done.1.refs_3_
  398.1 0.0 collective-permute-start.8
  398.2 0.9 collective-permute-done.2.refs_4_
  399.1 15.2 %shard_map.180 = (f32[2,384,3072]{2,1,0:T(8,128)}, f32[2,384,3072]{2,1,0:T(8,128)}, f32[2,384,3072]{2,1,0:T(8,128)}, f32[2,1536,768]{2,1,0:T(8,128)}, f32[2,1536...) custom-call(f32[2,8,128]{2,1,0:T(8,128)} %get-tuple-element.52.refs_, ...), custom_call_target="tpu_custom_call", output_to_operand_aliasing={{0}: (11, {}), {1}: (12, {}), {2}: (13, {}), {3}: (14, {}),... | custom-call | flops 471859200 | bytes 35389440 | tf_op jit(solution)/shard_map/pallas_call | solution.py:553
  414.3 0.0 collective-permute-start.3
  414.3 0.0 collective-permute-done.7.refs_2_
  414.3 0.5 collective-permute-start.4
  414.8 0.0 collective-permute-done.8.refs_3_
  414.8 0.0 collective-permute-done.5.refs_0_
  414.8 0.0 collective-permute-done.6.refs_1_
  414.8 6.0 %shard_map.181 = (bf16[2,768,3072]{2,1,0:T(8,128)(2,1)}, bf16[2,3072,768]{2,1,0:T(8,128)(2,1)}) custom-call(bf16[2,384,1536]{2,1,0:T(8,128)(2,1)} %collective-permute-done.5.refs_0_, bf16[12,128,768]{2,1,0:T(8,128)(2,1)} %collective-permute-done.6.refs_1_, ...), custom_call_target="tpu_custom_call", output_to_operand_aliasing={{0}: (4, {}), {1}: (5, {})} | custom-call | flops 353894400 | bytes 14155776 | tf_op jit(solution)/shard_map/pallas_call | solution.py:606
  420.8 0.0 collective-permute-done.3.refs_0_
  420.8 0.0 collective-permute-done.4.refs_1_
  420.9 2.6 shard_map.182
Async XLA Ops:
  353.9 28.7 %collective-permute-start = (f32[3,2,192,256]{3,2,1,0:T(8,128)}, f32[3,2,192,256]{3,2,1,0:T(8,128)}, u32[]{:S(2)}, u32[]{:S(2)}) collective-permute-start(f32[3,2,192,256]{3,2,1,0:T(8,128)} %get-tuple-element.53.refs_1_), channel_id=1, source_target_pairs={{0,4},{1,3},{2,6},{3,1},{4,0},{5,7},{6,2},{7,5}} | collective-permute-start | bytes 3538952 | tf_op jit(solution)/shard_map/ppermute | solution.py:635
  354.6 43.5 %collective-permute-start.1 = (f32[3,2,192,256]{3,2,1,0:T(8,128)}, f32[3,2,192,256]{3,2,1,0:T(8,128)}, u32[]{:S(2)}, u32[]{:S(2)}) collective-permute-start(f32[3,2,192,256]{3,2,1,0:T(8,128)} %get-tuple-element.53.refs_1_), channel_id=1, source_target_pairs={{0,2},{1,5},{2,0},{3,7},{4,6},{5,1},{6,4},{7,3}} | collective-permute-start | bytes 3538952 | tf_op jit(solution)/shard_map/ppermute | solution.py:635
  382.5 32.3 %collective-permute-start.5 = (bf16[2,384,1536]{2,1,0:T(8,128)(2,1)}, bf16[2,384,1536]{2,1,0:T(8,128)(2,1)}, u32[]{:S(2)}, u32[]{:S(2)}) collective-permute-start(bf16[2,384,1536]{2,1,0:T(8,128)(2,1)} %get-tuple-element.74), channel_id=1, source_target_pairs={{0,1},{1,0},{2,3},{3,2},{4,5},{5,4},{6,7},{7,6}} | collective-permute-start | bytes 7077896 | tf_op jit(solution)/shard_map/ppermute | solution.py:619
  382.6 16.5 %collective-permute-start.2 = (f32[3,2,192,256]{3,2,1,0:T(8,128)}, f32[3,2,192,256]{3,2,1,0:T(8,128)}, u32[]{:S(2)}, u32[]{:S(2)}) collective-permute-start(f32[3,2,192,256]{3,2,1,0:T(8,128)} %collective-permute-done.refs_2_), channel_id=1, source_target_pairs={{0,2},{1,5},{2,0},{3,7},{4,6},{5,1},{6,4},{7,3}} | collective-permute-start | bytes 3538952 | tf_op jit(solution)/shard_map/ppermute | solution.py:636
  383.5 31.4 %collective-permute-start.6 = (bf16[12,128,768]{2,1,0:T(8,128)(2,1)}, bf16[12,128,768]{2,1,0:T(8,128)(2,1)}, u32[]{:S(2)}, u32[]{:S(2)}) collective-permute-start(bf16[12,128,768]{2,1,0:T(8,128)(2,1)} %get-tuple-element.75), channel_id=1, source_target_pairs={{0,1},{1,0},{2,3},{3,2},{4,5},{5,4},{6,7},{7,6}} | collective-permute-start | bytes 7077896 | tf_op jit(solution)/shard_map/ppermute | solution.py:619
  397.6 16.7 %collective-permute-start.7 = (bf16[2,384,768]{2,1,0:T(8,128)(2,1)}, bf16[2,384,768]{2,1,0:T(8,128)(2,1)}, u32[]{:S(2)}, u32[]{:S(2)}) collective-permute-start(bf16[2,384,768]{2,1,0:T(8,128)(2,1)} %get-tuple-element.76), channel_id=1, source_target_pairs={{0,1},{1,0},{2,3},{3,2},{4,5},{5,4},{6,7},{7,6}} | collective-permute-start | bytes 3538952 | tf_op jit(solution)/shard_map/ppermute | solution.py:619
  398.1 16.7 %collective-permute-start.8 = (bf16[6,128,768]{2,1,0:T(8,128)(2,1)}, bf16[6,128,768]{2,1,0:T(8,128)(2,1)}, u32[]{:S(2)}, u32[]{:S(2)}) collective-permute-start(bf16[6,128,768]{2,1,0:T(8,128)(2,1)} %get-tuple-element.77), channel_id=1, source_target_pairs={{0,1},{1,0},{2,3},{3,2},{4,5},{5,4},{6,7},{7,6}} | collective-permute-start | bytes 3538952 | tf_op jit(solution)/shard_map/ppermute | solution.py:619
  414.3 6.6 %collective-permute-start.3 = (bf16[2,384,768]{2,1,0:T(8,128)(2,1)}, bf16[2,384,768]{2,1,0:T(8,128)(2,1)}, u32[]{:S(2)}, u32[]{:S(2)}) collective-permute-start(bf16[2,384,768]{2,1,0:T(8,128)(2,1)} %get-tuple-element.72), channel_id=1, source_target_pairs={{0,1},{1,0},{2,3},{3,2},{4,5},{5,4},{6,7},{7,6}} | collective-permute-start | bytes 3538952 | tf_op jit(solution)/shard_map/ppermute | solution.py:619
  414.3 6.5 %collective-permute-start.4 = (bf16[6,128,768]{2,1,0:T(8,128)(2,1)}, bf16[6,128,768]{2,1,0:T(8,128)(2,1)}, u32[]{:S(2)}, u32[]{:S(2)}) collective-permute-start(bf16[6,128,768]{2,1,0:T(8,128)(2,1)} %get-tuple-element.73), channel_id=1, source_target_pairs={{0,1},{1,0},{2,3},{3,2},{4,5},{5,4},{6,7},{7,6}} | collective-permute-start | bytes 3538952 | tf_op jit(solution)/shard_map/ppermute | solution.py:619
